TPU v7x, 1024 devices: a whole 4x8x16 slice. The times are simulated.
1024 devices in a mesh: fsdp: 32 (over z, x_hi), rep: 32 (over x_lo, y, core).
Axes of the slice: x: 4 (x_hi: 2, x_lo: 2; x = x_hi * 2 + x_lo), y: 8, z: 16, core: 2. Of those that a mesh axis runs over, the one named last changes fastest.
Arguments:
- expert_base_rows: bfloat16 [32, 1536, 4096], P('rep', None, 'fsdp'), may hold values from -6 to 6
- factor_in: bfloat16 [32, 1536, 32], P('rep'), may hold values from -6 to 6
- factor_out: bfloat16 [32, 32, 4096], P('rep', None, 'fsdp'), may hold values from -0.29882812 to 0.29882812
- source_group: int32 [4], replicated, may hold values from 0 to 31
- tp_order: int32 [32], replicated, may hold values from 0 to 31, each once
Outputs:
- rollout_weights: bfloat16 [32, 4, 1536, 4096], P('rep', None, 'fsdp')
Inputs may be any that keep to these rules, and one draw needn't show every extreme that they name: source_group[k] is the replica index along rep whose expert fills bucket k; entries may repeat. tp_order is a permutation of the 32 row blocks.
All inputs are finite; a program needn't handle non-finite values.
Results may differ from a plain program's by a relative error of at most 0.001.
Values may be sent and summed in bfloat16 or wider, within the bound.
No kernel may reach another device: no remote copies, remote signals or barrier semaphores. Data moves between devices by JAX's collectives and lax.ppermute only.
A program may use at most 64 MiB of HBM per device.

v0:
```python
import jax
import jax.numpy as jnp
from jax import lax
from jax.sharding import PartitionSpec as P

ADAPTER_SCALING = 2.0


def picked(shard, axis, root):
    return lax.dynamic_index_in_dim(lax.all_gather(shard, axis), root, 0, keepdims=False)


def body(expert_base_rows, factor_in, factor_out, source_group, tp_order):
    shard_count = lax.axis_size("fsdp")
    hidden_size = expert_base_rows.shape[1]
    slice_rows = hidden_size // shard_count
    adapter_delta = jnp.dot(factor_in[0], factor_out[0], preferred_element_type=jnp.float32)
    merged_weight = (
        expert_base_rows[0].astype(jnp.float32) + ADAPTER_SCALING * adapter_delta
    ).astype(jnp.bfloat16)
    blocks = jnp.take(
        merged_weight.reshape(shard_count, slice_rows, merged_weight.shape[1]), tp_order, axis=0
    )
    bucket = lax.all_to_all(blocks, "fsdp", split_axis=0, concat_axis=2, tiled=True)[0]
    published = []
    for slot_index in range(source_group.shape[0]):
        published.append(picked(bucket, "rep", source_group[slot_index]))
    return jnp.stack(published, axis=0)[None]


def solution(mesh):
    placed = (P("rep", None, "fsdp"), P("rep", None, None), P("rep", None, "fsdp"), P(), P())
    return jax.shard_map(
        body, mesh=mesh, in_specs=placed, out_specs=P("rep", None, "fsdp", None), check_vma=False
    )
```

profile of v0, /device:TPU:1, one launch (start us, length us, event | category | flops | bytes accessed | tf_op | source)
XLA Modules:
  0.0 149.3 jit_solution(1282562046290983107)
XLA Ops:
  6.5 0.0 copy-start
  6.5 0.0 all-gather.2.cloned.1.call-start
  6.5 0.7 compare_and_fusion
  7.2 0.7 compare_select_fusion
  7.9 0.0 copy-done
  7.9 1.3 fusion.1
  9.2 0.6 gather_fusion
  9.9 0.0 copy-start.1
  9.9 0.1 broadcast_select_fusion
  10.0 47.6 %all_to_all.18 = bf16[32,48,128]{2,1,0:T(8,128)(2,1)S(1)} all-to-all(bf16[32,48,128]{2,1,0:T(8,128)(2,1)S(1)} %broadcast_select_fusion), channel_id=1, replica_groups=mesh['fsdp'=32,'rep'=32] {'fsdp'}, dimensions={0} | all-to-all | bytes 786432 | tf_op jit(solution)/shard_map/all_to_all | solution.py:24
  57.6 0.8 copy_bitcast_fusion
  58.4 0.0 all-gather.2.cloned.1.call-update
  58.4 0.0 copy-done.1
  58.4 0.6 fusion.4
  66.5 73.1 %all-gather.2.cloned.1.call-done = bf16[32,48,4096]{2,1,0:T(8,128)(2,1)} async-done(((bf16[1,48,4096]{2,1,0:T(8,128)(2,1)}), bf16[32,48,4096]{2,1,0:T(8,128)(2,1)}) %all-gather.2.cloned.1.call-update) | async-done | bytes 12582928 | tf_op jit(solution)/shard_map/all_gather | solution.py:10
  139.6 1.5 constant_dynamic-slice_fusion.3
  141.1 1.3 maximum_bitcast_fusion
  (1 shorter events, 0.0 us)
Async XLA Ops:
  6.5 1.4 copy-start
  6.5 133.1 %all-gather.2.cloned.1.call-start = ((), (), s32[]{:S(2)}) async-start(), calls=%async_computation.1 | async-start | bytes 12976128 | tf_op jit(solution)/shard_map/all_gather | solution.py:10
  9.9 48.5 %copy-start.1 = (s32[4]{0:T(128)S(1)}, s32[4]{0:T(128)}, u32[]{:S(2)}) copy-start(s32[4]{0:T(128)} %param.8) | copy-start | bytes 52
Sparse Core Ops, SparseCore 0:
  58.5 81.0 all-gather.1
where the time goes:
time: 150 us; the launch traced here: 149 us
  waiting for transfers between devices  73.1 us (49%)
  blocking collectives  47.6 us (32%)
  between operations  20.9 us (14%)
  local copies, waits for them, and re-layouts  3.47 us (2%)
  other arithmetic  2.81 us (2%)
    all_gather x1, waiting for transfers between devices, picked(): lax.all_gather(shard, axis)  73.1 us
    all_to_all x1, blocking collectives, body(): lax.all_to_all(blocks, 'fsdp', split_axis=0, concat_axis=2, tiled=True)[0]  47.6 us
  transfers between devices with their start and end apart: 1, of which 1 were waited for; matrix products, arithmetic and copies ran while one was open for 0% of the time, Pallas kernels for 0%

commit v1 on v0

v1 whole, which is shorter than its diff:
```python
import jax
import jax.numpy as jnp
from jax import lax
from jax.sharding import Mesh, PartitionSpec as P

ADAPTER_SCALING = 2.0
CUT = {"z": 16, "xh": 2, "xl": 2, "y": 8, "c": 2}
FSDP, REP, EVERY = ("z", "xh"), ("xl", "y", "c"), ("z", "xh", "xl", "y", "c")
N = 32


def swing(r):
    xl, y, c = r // 16, (r // 2) % 8, r % 2
    return (c * 8 + y) * 2 + xl


def body(base, factor_in, factor_out, source_group, tp_order):
    f = lax.axis_index(FSDP)
    delta = jnp.dot(factor_in[0], factor_out[0], preferred_element_type=jnp.float32)
    merged = (base[0].astype(jnp.float32) + ADAPTER_SCALING * delta).astype(jnp.bfloat16)
    rows, width = merged.shape[0] // N, merged.shape[1]
    order = tp_order.at[f ^ swing(jnp.arange(N))].get(mode="promise_in_bounds")
    blocks = merged.reshape(N, rows, width).at[order].get(mode="promise_in_bounds")
    parts = lax.all_to_all(blocks, REP, split_axis=0, concat_axis=0, tiled=True)
    chosen = parts.at[source_group].get(mode="promise_in_bounds")
    pairs = [(s * N + r, (s ^ swing(r)) * N + r) for s in range(N) for r in range(N)]
    piece = lax.ppermute(chosen, EVERY, pairs)
    copies = jnp.broadcast_to(piece[None], (16, *piece.shape))
    half = lax.all_to_all(copies, ("xl", "y"), split_axis=0, concat_axis=0, tiled=True)
    other = lax.ppermute(half, "c", [(0, 1), (1, 0)])
    c = lax.axis_index("c")
    far = jnp.arange(N) ^ f
    at = (far % 2) * 8 + (far // 2) % 8
    both = jnp.concatenate([half, other], axis=0)
    at = at + 16 * ((far // 16) ^ c)
    wide = both.at[at].get(mode="promise_in_bounds")
    return wide.transpose(1, 2, 0, 3).reshape(1, *piece.shape[:2], N * width)


def solution(mesh):
    fine = Mesh(mesh.devices.reshape(tuple(CUT.values())), tuple(CUT))
    placed = (P(REP, None, FSDP), P(REP, None, None), P(REP, None, FSDP), P(), P())
    return jax.shard_map(
        body, mesh=fine, in_specs=placed, out_specs=P(REP, None, FSDP, None), check_vma=False
    )
```

time: 150 us -> 84.7 us (0.56)
  waiting for transfers between devices: 73.1 us -> 18.6 us
  starting transfers between devices: 0.01 us -> 33.4 us
  blocking collectives: 47.6 us -> 23.3 us
  between operations: 20.9 us -> 0.12 us
  local copies, waits for them, and re-layouts: 3.47 us -> 7.36 us
  other arithmetic: 2.81 us -> 0.22 us
    all_gather x1 -> x0, waiting for transfers between devices: 73.1 us -> none  [picked(): lax.all_gather(shard, axis)]
    all_to_all x1, blocking collectives: 47.6 us -> 23.3 us  [body(): lax.all_to_all(copies, ('xl', 'y'), split_axis=0, concat_axis=0, tiled=True)]
    all_to_all x0 -> x1, starting transfers between devices: none -> 17.6 us  [body(): parts = lax.all_to_all(blocks, REP, split_axis=0, concat_axis=0, tiled=True)]
    ppermute x0 -> x2, starting transfers between devices: none -> 15.8 us  [the longest x1 11 us: body(): piece = lax.ppermute(chosen, EVERY, pairs)]
    all_to_all x0 -> x1, waiting for transfers between devices: none -> 14.2 us  [body(): parts = lax.all_to_all(blocks, REP, split_axis=0, concat_axis=0, tiled=True)]
    ppermute x0 -> x2, waiting for transfers between devices: none -> 4.4 us  [the longest x1 2.56 us: body(): piece = lax.ppermute(chosen, EVERY, pairs)]
    gather x1 -> x4, local copies, waits for them, and re-layouts: 0.62 us -> 4.14 us  [the longest x1 1.38 us: body(): order = tp_order.at[f ^ swing(jnp.arange(N))].get(mode='promise_in_bounds')]
    reshape x0 -> x1, local copies, waits for them, and re-layouts: none -> 2.06 us  [body(): return wide.transpose(1, 2, 0, 3).reshape(1, *piece.shape[:2], N * width)]
  transfers between devices with their start and end apart: 1 -> 3, of which waited for: 1 -> 3; matrix products, arithmetic and copies ran while one was open for 0% -> 0% of each run, Pallas kernels for 0% -> 0%
where the time goes in v1:
time: 84.7 us; the launch traced here: 84.3 us
  starting transfers between devices  33.4 us (39%)
  blocking collectives  23.3 us (28%)
  waiting for transfers between devices  18.6 us (22%)
  local copies, waits for them, and re-layouts  7.36 us (9%)
  matrix products  1.33 us (2%)
    all_to_all x1, blocking collectives, body(): lax.all_to_all(copies, ('xl', 'y'), split_axis=0, concat_axis=0, tiled=True)  23.3 us
    all_to_all x1, starting transfers between devices, body(): parts = lax.all_to_all(blocks, REP, split_axis=0, concat_axis=0, tiled=True)  17.6 us
    all_to_all x1, waiting for transfers between devices, body(): parts = lax.all_to_all(blocks, REP, split_axis=0, concat_axis=0, tiled=True)  14.2 us
    ppermute x1, starting transfers between devices, body(): piece = lax.ppermute(chosen, EVERY, pairs)  11 us
    ppermute x1, starting transfers between devices, body(): other = lax.ppermute(half, 'c', [(0, 1), (1, 0)])  4.82 us
    ppermute x1, waiting for transfers between devices, body(): piece = lax.ppermute(chosen, EVERY, pairs)  2.56 us
    reshape x1, local copies, waits for them, and re-layouts, body(): return wide.transpose(1, 2, 0, 3).reshape(1, *piece.shape[:2], N * width)  2.06 us
    ppermute x1, waiting for transfers between devices, body(): other = lax.ppermute(half, 'c', [(0, 1), (1, 0)])  1.85 us
  transfers between devices with their start and end apart: 3, of which 3 were waited for; matrix products, arithmetic and copies ran while one was open for 0% of the time, Pallas kernels for 0%

profile of v1, /device:TPU:1, one launch (start us, length us, event | category | flops | bytes accessed | tf_op | source)
XLA Modules:
  0.0 84.3 jit_solution(12176762130199574149)
XLA Ops:
  0.0 0.0 copy-start
  0.0 0.0 copy-start.1
  0.0 1.4 %gather_fusion = s32[32]{0:T(128)S(1)} fusion(s32[32]{0:T(128)} %param.9, s32[1024]{0:T(1024)S(1)} %pad_clamp_fusion.3), kind=kCustom, calls=%fused_computation | custom fusion | bytes 384 | tf_op jit(solution)/shard_map/gather | solution.py:22
  1.4 0.0 copy-done
  1.5 1.3 %fusion.1 = bf16[1536,128]{1,0:T(8,128)(2,1)S(1)} fusion(bf16[1,1536,128]{2,1,0:T(8,128)(2,1)} %param.5, bf16[1,1536,32]{1,2,0:T(8,128)(2,1)S(1)} %copy-done, bf16[1,32,128]{2,1,0:T(8,128)(2,1)} %param.7), kind=kOutput, calls=%fused_computation.6 | convolution fusion | flops 13369344 | bytes 892928 | tf_op jit(solution)/shard_map/dot_general | solution.py:19
  2.8 1.3 %gather_fusion.1 = bf16[32,48,128]{2,1,0:T(8,128)(2,1)} fusion(bf16[32,48,128]{2,1,0:T(8,128)(2,1)S(1)} %bitcast.22, s32[1024]{0:T(1024)S(1)} %pad_clamp_fusion.2), kind=kCustom, calls=%fused_computation.1 | custom fusion | bytes 786560 | tf_op jit(solution)/shard_map/gather | solution.py:23
  4.1 17.6 %all-to-all-start = ((bf16[32,48,128]{2,1,0:T(8,128)(2,1)}), bf16[32,48,128]{2,1,0:T(8,128)(2,1)S(1)}, u32[]{:S(2)}, u32[]{:S(2)}) async-start(bf16[32,48,128]{2,1,0:T(8,128)(2,1)} %gather_fusion.1), calls=%async_computation | async-start | bytes 786432 | tf_op jit(solution)/shard_map/all_to_all | solution.py:24
  21.8 0.0 copy-done.1
  21.8 14.2 %all-to-all-done = bf16[32,48,128]{2,1,0:T(8,128)(2,1)S(1)} async-done(((bf16[32,48,128]{2,1,0:T(8,128)(2,1)}), bf16[32,48,128]{2,1,0:T(8,128)(2,1)S(1)}, u32[]{:S(2)}, u32[]{:S(2)}) %all-to-all-start) | async-done | bytes 393248 | tf_op jit(solution)/shard_map/all_to_all | solution.py:24
  36.0 0.6 gather_fusion.2
  36.5 11.0 %collective-permute-start = (bf16[4,48,128]{2,1,0:T(8,128)(2,1)S(1)}, bf16[4,48,128]{2,1,0:T(8,128)(2,1)S(1)}, u32[]{:S(2)}, u32[]{:S(2)}) collective-permute-start(bf16[4,48,128]{2,1,0:T(8,128)(2,1)S(1)} %gather_fusion.2), channel_id=1, source_target_pairs={{0,0},{1,513},{2,66},{3,579},{4,132},{5,645},{6,198},{7,711},{8,26... | collective-permute-start | bytes 147464 | tf_op jit(solution)/shard_map/ppermute | solution.py:27
  47.5 2.6 %collective-permute-done = bf16[4,48,128]{2,1,0:T(8,128)(2,1)S(1)} collective-permute-done((bf16[4,48,128]{2,1,0:T(8,128)(2,1)S(1)}, bf16[4,48,128]{2,1,0:T(8,128)(2,1)S(1)}, u32[]{:S(2)}, u32[]{:S(2)}) %collective-permute-start) | collective-permute-done | bytes 49184 | tf_op jit(solution)/shard_map/ppermute | solution.py:27
  50.1 0.1 broadcast_in_dim.5
  50.2 23.3 %all_to_all.10 = bf16[16,4,48,128]{3,2,1,0:T(8,128)(2,1)S(1)} all-to-all(bf16[16,4,48,128]{3,2,1,0:T(8,128)(2,1)S(1)} %broadcast_in_dim.5), channel_id=1, replica_groups=mesh['z'=16,'xh'=2,'xl'=2,'y'=8,'c'=2] {'xl','y'}, dimensions={0} | all-to-all | bytes 1572864 | tf_op jit(solution)/shard_map/all_to_all | solution.py:29
  73.5 4.8 %collective-permute-start.1 = (bf16[16,4,48,128]{3,2,1,0:T(8,128)(2,1)S(1)}, bf16[16,4,48,128]{3,2,1,0:T(8,128)(2,1)S(1)}, u32[]{:S(2)}, u32[]{:S(2)}) collective-permute-start(bf16[16,4,48,128]{3,2,1,0:T(8,128)(2,1)S(1)} %all_to_all.10), channel_id=1, source_target_pairs={{0,1},{1,0},{2,3},{3,2},{4,5},{5,4},{6,7},{7,6},{8,9},{9,8},{10,11... | collective-permute-start | bytes 2359304 | tf_op jit(solution)/shard_map/ppermute | solution.py:30
  78.4 1.8 %collective-permute-done.1 = bf16[16,4,48,128]{3,2,1,0:T(8,128)(2,1)S(1)} collective-permute-done((bf16[16,4,48,128]{3,2,1,0:T(8,128)(2,1)S(1)}, bf16[16,4,48,128]{3,2,1,0:T(8,128)(2,1)S(1)}, u32[]{:S(2)}, u32[]{:S(2)}) %collective-permute-start.1) | collective-permute-done | bytes 786464 | tf_op jit(solution)/shard_map/ppermute | solution.py:30
  80.2 0.1 pad_maximum_fusion
  80.4 0.9 %gather_fusion.3 = bf16[32,4,48,128]{3,2,1,0:T(8,128)(2,1)S(1)} fusion(bf16[32,4,48,128]{3,2,1,0:T(8,128)(2,1)S(1)} %pad_maximum_fusion, s32[1024]{0:T(1024)S(1)} %pad_clamp_fusion), kind=kCustom, calls=%fused_computation.3 | custom fusion | bytes 3145856 | tf_op jit(solution)/shard_map/gather | solution.py:36
  81.2 1.0 %copy.6 = bf16[4,48,32,128]{3,2,1,0:T(8,128)(2,1)S(1)} copy(bf16[4,48,32,128]{3,1,0,2:T(8,128)(2,1)S(1)} %bitcast.21) | data formatting | bytes 3145728 | tf_op jit(solution)/shard_map/transpose | solution.py:37
  82.3 2.1 %reshape.311 = bf16[1,4,48,4096]{3,2,1,0:T(8,128)(2,1)} reshape(bf16[4,48,32,128]{3,2,1,0:T(8,128)(2,1)S(1)} %copy.6) | data formatting | bytes 3145728 | tf_op jit(solution)/shard_map/reshape | solution.py:37
  (8 shorter events, 0.1 us)
Async XLA Ops:
  0.0 1.4 %copy-start = (bf16[1,1536,32]{1,2,0:T(8,128)(2,1)S(1)}, bf16[1,1536,32]{1,2,0:T(8,128)(2,1)}, u32[]{:S(2)}) copy-start(bf16[1,1536,32]{1,2,0:T(8,128)(2,1)} %param.6) | copy-start | bytes 294916
  0.0 21.8 %copy-start.1 = (s32[4]{0:T(128)S(1)}, s32[4]{0:T(128)}, u32[]{:S(2)}) copy-start(s32[4]{0:T(128)} %param.8) | copy-start | bytes 52
  4.1 31.8 %all-to-all-start = ((bf16[32,48,128]{2,1,0:T(8,128)(2,1)}), bf16[32,48,128]{2,1,0:T(8,128)(2,1)S(1)}, u32[]{:S(2)}, u32[]{:S(2)}) async-start(bf16[32,48,128]{2,1,0:T(8,128)(2,1)} %gather_fusion.1), calls=%async_computation | async-start | bytes 786432 | tf_op jit(solution)/shard_map/all_to_all | solution.py:24
  36.5 13.5 %collective-permute-start = (bf16[4,48,128]{2,1,0:T(8,128)(2,1)S(1)}, bf16[4,48,128]{2,1,0:T(8,128)(2,1)S(1)}, u32[]{:S(2)}, u32[]{:S(2)}) collective-permute-start(bf16[4,48,128]{2,1,0:T(8,128)(2,1)S(1)} %gather_fusion.2), channel_id=1, source_target_pairs={{0,0},{1,513},{2,66},{3,579},{4,132},{5,645},{6,198},{7,711},{8,26... | collective-permute-start | bytes 147464 | tf_op jit(solution)/shard_map/ppermute | solution.py:27
  73.5 6.7 %collective-permute-start.1 = (bf16[16,4,48,128]{3,2,1,0:T(8,128)(2,1)S(1)}, bf16[16,4,48,128]{3,2,1,0:T(8,128)(2,1)S(1)}, u32[]{:S(2)}, u32[]{:S(2)}) collective-permute-start(bf16[16,4,48,128]{3,2,1,0:T(8,128)(2,1)S(1)} %all_to_all.10), channel_id=1, source_target_pairs={{0,1},{1,0},{2,3},{3,2},{4,5},{5,4},{6,7},{7,6},{8,9},{9,8},{10,11... | collective-permute-start | bytes 2359304 | tf_op jit(solution)/shard_map/ppermute | solution.py:30

commit v2 on v1

v2 whole, which is shorter than its diff:
```python
import jax
import jax.numpy as jnp
import numpy as np
from jax import lax
from jax.sharding import Mesh, PartitionSpec as P

ADAPTER_SCALING = 2.0
CUT = {"z": 16, "xh": 2, "xl": 2, "y": 8, "c": 2}
FSDP, REP = ("z", "xh"), ("xl", "y", "c")
SWING = np.array(
    [[0, 8], [1, 9], [2, 10], [3, 11], [4, 7], [12, 15], [5, 6], [13, 14]], np.int32
)


def body(base, factor_in, factor_out, source_group, tp_order):
    z = lax.axis_index("z")
    rows, width = base.shape[1] // 64, base.shape[2]
    delta = jnp.dot(factor_in[0], factor_out[0], preferred_element_type=jnp.float32)
    merged = (base[0].astype(jnp.float32) + ADAPTER_SCALING * delta).astype(jnp.bfloat16)
    xh, xl, y, c = np.meshgrid(*(np.arange(n) for n in (2, 2, 8, 2)), indexing="ij")
    to = (z ^ jnp.asarray(SWING[y, c].ravel())) * 2 + jnp.asarray(xh.ravel())
    order = tp_order.at[to].get(mode="promise_in_bounds") * 2 + jnp.asarray(xl.ravel())
    halves = merged.reshape(64, rows, width).at[order].get(mode="promise_in_bounds")
    parts = lax.all_to_all(halves, ("xh",) + REP, split_axis=0, concat_axis=0, tiled=True)
    pick = jnp.concatenate([source_group, source_group + 32])
    chosen = parts.at[pick].get(mode="promise_in_bounds")
    pairs = [
        ((s * 8 + y) * 2 + c, ((s ^ int(SWING[y, c])) * 8 + y) * 2 + c)
        for s in range(16)
        for y in range(8)
        for c in range(2)
    ]
    piece = lax.ppermute(chosen, ("z", "y", "c"), pairs)
    copies = jnp.broadcast_to(piece[None], (16, *piece.shape))
    half = lax.all_to_all(copies, ("xl", "y"), split_axis=0, concat_axis=0, tiled=True)
    other = lax.ppermute(half, "c", [(0, 1), (1, 0)])
    core = lax.axis_index("c")
    both = jnp.concatenate([half, other], axis=0).reshape(2, 2, 8, 2, 4, rows, width)
    back = np.zeros((16, 2), np.int32)
    for y in range(8):
        for c in range(2):
            back[SWING[y, c]] = (y, c)
    far = jnp.asarray(back)[jnp.arange(16) ^ z]
    wide = both.transpose(0, 2, 1, 3, 4, 5, 6).reshape(16, 2, 2, 4, rows, width)
    wide = wide.at[(far[:, 1] ^ core) * 8 + far[:, 0]].get(mode="promise_in_bounds")
    return wide.transpose(3, 1, 4, 0, 2, 5).reshape(1, 4, 2 * rows, 32 * width)


def solution(mesh):
    fine = Mesh(mesh.devices.reshape(tuple(CUT.values())), tuple(CUT))
    placed = (P(REP, None, FSDP), P(REP, None, None), P(REP, None, FSDP), P(), P())
    return jax.shard_map(
        body, mesh=fine, in_specs=placed, out_specs=P(REP, None, FSDP, None), check_vma=False
    )
```

time: 84.7 us -> 89.1 us (1.052)
  blocking collectives: 23.3 us -> 26.3 us
  other arithmetic: 0.22 us -> 1.94 us
  local copies, waits for them, and re-layouts: 7.36 us -> 9.03 us
  waiting for transfers between devices: 18.6 us -> 17.4 us
    all_to_all x1, blocking collectives: 23.3 us -> 26.3 us  [body(): lax.all_to_all(copies, ('xl', 'y'), split_axis=0, concat_axis=0, tiled=True)]
    ppermute x1, starting transfers between devices: 4.82 us -> 1.91 us  [body(): other = lax.ppermute(half, 'c', [(0, 1), (1, 0)])]
    select_n x4 -> x5, other arithmetic: 0.05 us -> 1.76 us  [the longest x1 0.71 us: body(): tp_order.at[to].get(mode='promise_in_bounds') * 2 + jnp.asarray(xl.ravel())]
    ppermute x1, starting transfers between devices: 11 us -> 12.4 us  [body(): piece = lax.ppermute(chosen, ('z', 'y', 'c'), pairs)]
    ppermute x1, waiting for transfers between devices: 2.56 us -> 1.51 us  [body(): piece = lax.ppermute(chosen, ('z', 'y', 'c'), pairs)]
    gather x4 -> x5, local copies, waits for them, and re-layouts: 4.14 us -> 4.78 us  [the longest x1 1.43 us: body(): tp_order.at[to].get(mode='promise_in_bounds') * 2 + jnp.asarray(xl.ravel())]
  transfers between devices with their start and end apart: 3 -> 3, of which waited for: 3 -> 3; matrix products, arithmetic and copies ran while one was open for 0% -> 1% of each run, Pallas kernels for 0% -> 0%
where the time goes in v2:
time: 89.1 us; the launch traced here: 88.7 us
  starting transfers between devices  32.6 us (37%)
  blocking collectives  26.3 us (30%)
  waiting for transfers between devices  17.4 us (20%)
  local copies, waits for them, and re-layouts  9.03 us (10%)
  other arithmetic  1.94 us (2%)
  matrix products  1.32 us (1%)
    all_to_all x1, blocking collectives, body(): lax.all_to_all(copies, ('xl', 'y'), split_axis=0, concat_axis=0, tiled=True)  26.3 us
    all_to_all x1, starting transfers between devices, body(): lax.all_to_all(halves, ('xh',) + REP, split_axis=0, concat_axis=0, tiled=...  18.3 us
    all_to_all x1, waiting for transfers between devices, body(): lax.all_to_all(halves, ('xh',) + REP, split_axis=0, concat_axis=0, tiled=...  14.6 us
    ppermute x1, starting transfers between devices, body(): piece = lax.ppermute(chosen, ('z', 'y', 'c'), pairs)  12.4 us
    reshape x1, local copies, waits for them, and re-layouts, body(): return wide.transpose(3, 1, 4, 0, 2, 5).reshape(1, 4, 2 * rows, 32 * width)  2.39 us
    ppermute x1, starting transfers between devices, body(): other = lax.ppermute(half, 'c', [(0, 1), (1, 0)])  1.91 us
  transfers between devices with their start and end apart: 3, of which 3 were waited for; matrix products, arithmetic and copies ran while one was open for 1% of the time, Pallas kernels for 0%

profile of v2, /device:TPU:1, one launch (start us, length us, event | category | flops | bytes accessed | tf_op | source)
XLA Modules:
  0.0 88.7 jit_solution(11271541474454213286)
XLA Ops:
  0.0 0.0 copy-start
  0.0 0.0 copy-start.2
  0.0 0.7 compare_select_fusion.4
  0.7 1.4 %gather_fusion = s32[64]{0:T(128)S(1)} fusion(s32[32]{0:T(128)} %param.13, s32[1024]{0:T(1024)S(1)} %pad_clamp_fusion.4), kind=kCustom, calls=%fused_computation | custom fusion | bytes 768 | tf_op jit(solution)/shard_map/gather | solution.py:22
  2.2 0.7 compare_select_fusion.3
  2.8 0.0 copy-done
  2.8 1.3 %fusion.1 = bf16[1536,128]{1,0:T(8,128)(2,1)S(1)} fusion(bf16[1,1536,128]{2,1,0:T(8,128)(2,1)} %param.9, bf16[1,1536,32]{1,2,0:T(8,128)(2,1)S(1)} %copy-done, bf16[1,32,128]{2,1,0:T(8,128)(2,1)} %param.11), kind=kOutput, calls=%fused_computation.7 | convolution fusion | flops 13369344 | bytes 892928 | tf_op jit(solution)/shard_map/dot_general | solution.py:18
  4.2 1.4 %gather_fusion.1 = bf16[64,24,128]{2,1,0:T(8,128)(2,1)} fusion(bf16[64,24,128]{2,1,0:T(8,128)(2,1)S(1)} %bitcast.23, s32[1024]{0:T(1024)S(1)} %pad_clamp_fusion.3), kind=kCustom, calls=%fused_computation.1 | custom fusion | bytes 786688 | tf_op jit(solution)/shard_map/gather | solution.py:23
  5.5 0.0 copy-start.1
  5.6 18.3 %all-to-all-start = ((bf16[64,24,128]{2,1,0:T(8,128)(2,1)}), bf16[64,24,128]{2,1,0:T(8,128)(2,1)S(1)}, u32[]{:S(2)}, u32[]{:S(2)}) async-start(bf16[64,24,128]{2,1,0:T(8,128)(2,1)} %gather_fusion.1), calls=%async_computation | async-start | bytes 786432 | tf_op jit(solution)/shard_map/all_to_all | solution.py:24
  23.9 0.0 copy-done.2
  23.9 0.1 fusion.7
  24.0 14.6 %all-to-all-done = bf16[64,24,128]{2,1,0:T(8,128)(2,1)S(1)} async-done(((bf16[64,24,128]{2,1,0:T(8,128)(2,1)}), bf16[64,24,128]{2,1,0:T(8,128)(2,1)S(1)}, u32[]{:S(2)}, u32[]{:S(2)}) %all-to-all-start) | async-done | bytes 393248 | tf_op jit(solution)/shard_map/all_to_all | solution.py:24
  38.5 0.6 gather_fusion.2
  39.1 12.4 %collective-permute-start = (bf16[8,24,128]{2,1,0:T(8,128)(2,1)S(1)}, bf16[8,24,128]{2,1,0:T(8,128)(2,1)S(1)}, u32[]{:S(2)}, u32[]{:S(2)}) collective-permute-start(bf16[8,24,128]{2,1,0:T(8,128)(2,1)S(1)} %gather_fusion.2), channel_id=1, source_target_pairs={{0,0},{1,513},{2,66},{3,579},{4,132},{5,645},{6,198},{7,711},{8,26... | collective-permute-start | bytes 147464 | tf_op jit(solution)/shard_map/ppermute | solution.py:33
  51.5 1.5 %collective-permute-done = bf16[8,24,128]{2,1,0:T(8,128)(2,1)S(1)} collective-permute-done((bf16[8,24,128]{2,1,0:T(8,128)(2,1)S(1)}, bf16[8,24,128]{2,1,0:T(8,128)(2,1)S(1)}, u32[]{:S(2)}, u32[]{:S(2)}) %collective-permute-start) | collective-permute-done | bytes 49184 | tf_op jit(solution)/shard_map/ppermute | solution.py:33
  53.0 0.1 broadcast_in_dim.8
  53.2 26.3 %all_to_all.10 = bf16[16,8,24,128]{3,2,1,0:T(8,128)(2,1)S(1)} all-to-all(bf16[16,8,24,128]{3,2,1,0:T(8,128)(2,1)S(1)} %broadcast_in_dim.8), channel_id=1, replica_groups=mesh['z'=16,'xh'=2,'xl'=2,'y'=8,'c'=2] {'xl','y'}, dimensions={0} | all-to-all | bytes 1572864 | tf_op jit(solution)/shard_map/all_to_all | solution.py:35
  79.5 1.9 %collective-permute-start.1 = (bf16[16,8,24,128]{3,2,1,0:T(8,128)(2,1)S(1)}, bf16[16,8,24,128]{3,2,1,0:T(8,128)(2,1)S(1)}, u32[]{:S(2)}, u32[]{:S(2)}) collective-permute-start(bf16[16,8,24,128]{3,2,1,0:T(8,128)(2,1)S(1)} %all_to_all.10), channel_id=1, source_target_pairs={{0,1},{1,0},{2,3},{3,2},{4,5},{5,4},{6,7},{7,6},{8,9},{9,8},{10,11... | collective-permute-start | bytes 2359304 | tf_op jit(solution)/shard_map/ppermute | solution.py:36
  81.4 0.1 fusion.3
  81.5 0.0 copy-done.1
  81.5 0.6 gather_fusion.3
  82.1 0.2 fusion.4
  82.3 1.4 %collective-permute-done.1 = bf16[16,8,24,128]{3,2,1,0:T(8,128)(2,1)S(1)} collective-permute-done((bf16[16,8,24,128]{3,2,1,0:T(8,128)(2,1)S(1)}, bf16[16,8,24,128]{3,2,1,0:T(8,128)(2,1)S(1)}, u32[]{:S(2)}, u32[]{:S(2)}) %collective-permute-start.1) | collective-permute-done | bytes 786464 | tf_op jit(solution)/shard_map/ppermute | solution.py:36
  83.6 0.1 pad_maximum_fusion
  83.8 0.3 copy.10
  84.1 0.9 gather_fusion.4
  84.9 1.4 %copy.11 = bf16[4,2,24,16,2,128]{5,4,3,2,1,0:T(2,128)(2,1)S(1)} copy(bf16[4,2,24,16,2,128]{5,2,0,4,1,3:T(8,128)(2,1)S(1)} %bitcast.22) | data formatting | bytes 3145728 | tf_op jit(solution)/shard_map/transpose | solution.py:46
  86.4 2.4 %reshape.117 = bf16[1,4,48,4096]{3,2,1,0:T(8,128)(2,1)} reshape(bf16[4,2,24,16,2,128]{5,4,3,2,1,0:T(2,128)(2,1)S(1)} %copy.11) | data formatting | bytes 3145728 | tf_op jit(solution)/shard_map/reshape | solution.py:46
  (6 shorter events, 0.0 us)
Async XLA Ops:
  0.0 2.8 %copy-start = (bf16[1,1536,32]{1,2,0:T(8,128)(2,1)S(1)}, bf16[1,1536,32]{1,2,0:T(8,128)(2,1)}, u32[]{:S(2)}) copy-start(bf16[1,1536,32]{1,2,0:T(8,128)(2,1)} %param.10) | copy-start | bytes 294916
  0.0 23.9 %copy-start.2 = (s32[4]{0:T(128)S(1)}, s32[4]{0:T(128)}, u32[]{:S(2)}) copy-start(s32[4]{0:T(128)} %param.12) | copy-start | bytes 52
  5.5 76.0 %copy-start.1 = (s32[16,2]{1,0:T(8,128)S(1)}, s32[16,2]{1,0:T(8,128)}, u32[]{:S(2)}) copy-start(s32[16,2]{1,0:T(8,128)} %constant.39.clone) | copy-start | bytes 388
  5.6 33.0 %all-to-all-start = ((bf16[64,24,128]{2,1,0:T(8,128)(2,1)}), bf16[64,24,128]{2,1,0:T(8,128)(2,1)S(1)}, u32[]{:S(2)}, u32[]{:S(2)}) async-start(bf16[64,24,128]{2,1,0:T(8,128)(2,1)} %gather_fusion.1), calls=%async_computation | async-start | bytes 786432 | tf_op jit(solution)/shard_map/all_to_all | solution.py:24
  39.1 13.9 %collective-permute-start = (bf16[8,24,128]{2,1,0:T(8,128)(2,1)S(1)}, bf16[8,24,128]{2,1,0:T(8,128)(2,1)S(1)}, u32[]{:S(2)}, u32[]{:S(2)}) collective-permute-start(bf16[8,24,128]{2,1,0:T(8,128)(2,1)S(1)} %gather_fusion.2), channel_id=1, source_target_pairs={{0,0},{1,513},{2,66},{3,579},{4,132},{5,645},{6,198},{7,711},{8,26... | collective-permute-start | bytes 147464 | tf_op jit(solution)/shard_map/ppermute | solution.py:33
  79.5 4.2 %collective-permute-start.1 = (bf16[16,8,24,128]{3,2,1,0:T(8,128)(2,1)S(1)}, bf16[16,8,24,128]{3,2,1,0:T(8,128)(2,1)S(1)}, u32[]{:S(2)}, u32[]{:S(2)}) collective-permute-start(bf16[16,8,24,128]{3,2,1,0:T(8,128)(2,1)S(1)} %all_to_all.10), channel_id=1, source_target_pairs={{0,1},{1,0},{2,3},{3,2},{4,5},{5,4},{6,7},{7,6},{8,9},{9,8},{10,11... | collective-permute-start | bytes 2359304 | tf_op jit(solution)/shard_map/ppermute | solution.py:36

commit v3 on v1

v3 whole, which is shorter than its diff:
```python
import jax
import jax.numpy as jnp
from jax import lax
from jax.experimental import pallas as pl
from jax.experimental.pallas import tpu as pltpu
from jax.sharding import Mesh, PartitionSpec as P

ADAPTER_SCALING = 2.0
CUT = {"z": 16, "xh": 2, "xl": 2, "y": 8, "c": 2}
FSDP, REP = ("z", "xh"), ("xl", "y", "c")
EVERY = FSDP + REP
N = 32
SCALAR = pl.BlockSpec(memory_space=pltpu.SMEM)
FAR = pl.BlockSpec(memory_space=pl.ANY)
LOCAL = pl.BlockSpec(memory_space=pltpu.VMEM)


def swing(r):
    xl, y, c = r // 16, (r // 2) % 8, r % 2
    return (c * 8 + y) * 2 + xl


def merge_kernel(me, tp_order, base, left, right, out, tp, rows_in, a, b, merged, sems, tp_sem):
    step = 384
    parts = [pl.ds(at, step) for at in range(0, base.shape[0], step)]
    moves = [
        pltpu.make_async_copy(left, a, sems.at[0]),
        pltpu.make_async_copy(right, b, sems.at[1]),
    ] + [
        pltpu.make_async_copy(base.at[part], rows_in.at[part], sems.at[2 + i])
        for i, part in enumerate(parts)
    ]
    order = pltpu.make_async_copy(tp_order, tp, tp_sem)
    order.start()
    for move in moves:
        move.start()
    for move in moves[:2]:
        move.wait()
    for part, move in zip(parts, moves[2:]):
        delta = lax.dot_general(
            a[:, part], b[...], (((0,), (0,)), ((), ())), preferred_element_type=jnp.float32
        )
        move.wait()
        wide = rows_in[part, :].astype(jnp.float32) + ADAPTER_SCALING * delta
        merged[part, :] = wide.astype(jnp.bfloat16)
    order.wait()
    rows = out.shape[1]
    for r in range(N):
        at = pl.multiple_of(tp[me[0] ^ swing(r)] * rows, 16)
        out[r] = merged[pl.ds(at, rows), :]


def order_kernel(me, own, other, out, wide, sems):
    width = own.shape[-1]
    for k in range(own.shape[1]):
        for at in range(own.shape[0]):
            code = (at % 8) * 2 + at // 8
            for side, ref in enumerate((own, other)):
                lane = pl.multiple_of((me[side] ^ code) * width, width)
                wide[k, :, pl.ds(lane, width)] = ref[at, k]
        pltpu.make_async_copy(wide.at[k], out.at[k], sems.at[k]).start()
    for k in range(own.shape[1]):
        pltpu.make_async_copy(wide.at[k], out.at[k], sems.at[k]).wait()


def body(base, factor_in, factor_out, source_group, tp_order):
    f, c = lax.axis_index(FSDP), lax.axis_index("c")
    rows, width = base.shape[1] // N, base.shape[2]
    blocks = pl.pallas_call(
        merge_kernel,
        out_shape=jax.ShapeDtypeStruct((N, rows, width), jnp.bfloat16),
        in_specs=[SCALAR] + [FAR] * 4,
        out_specs=LOCAL,
        scratch_shapes=[
            pltpu.SMEM((N,), jnp.int32),
            pltpu.VMEM((N * rows, width), jnp.bfloat16),
            pltpu.VMEM(factor_in.shape[:0:-1], jnp.bfloat16),
            pltpu.VMEM(factor_out.shape[1:], jnp.bfloat16),
            pltpu.VMEM((N * rows, width), jnp.bfloat16),
            pltpu.SemaphoreType.DMA((6,)),
            pltpu.SemaphoreType.DMA(()),
        ],
        name="merge",
    )(f[None], tp_order, base[0], factor_in[0].T, factor_out[0])
    parts = lax.all_to_all(blocks, REP, split_axis=0, concat_axis=0, tiled=True)
    chosen = parts.at[source_group].get(mode="promise_in_bounds")
    pairs = [(s * N + r, (s ^ swing(r)) * N + r) for s in range(N) for r in range(N)]
    piece = lax.ppermute(chosen, EVERY, pairs)
    copies = jnp.broadcast_to(piece[None], (16, *piece.shape))
    half = lax.all_to_all(copies, ("xl", "y"), split_axis=0, concat_axis=0, tiled=True)
    other = lax.ppermute(half, "c", [(0, 1), (1, 0)])
    out = pl.pallas_call(
        order_kernel,
        out_shape=jax.ShapeDtypeStruct((*piece.shape[:2], N * width), jnp.bfloat16),
        in_specs=[SCALAR, LOCAL, LOCAL],
        out_specs=FAR,
        scratch_shapes=[
            pltpu.VMEM((*piece.shape[:2], N * width), jnp.bfloat16),
            pltpu.SemaphoreType.DMA((piece.shape[0],)),
        ],
        compiler_params=pltpu.CompilerParams(vmem_limit_bytes=8 << 20),
        name="order",
    )(jnp.stack([f ^ (c * 16), f ^ ((1 - c) * 16)]), half, other)
    return out[None]


def solution(mesh):
    fine = Mesh(mesh.devices.reshape(tuple(CUT.values())), tuple(CUT))
    placed = (P(REP, None, FSDP), P(REP, None, None), P(REP, None, FSDP), P(), P())
    return jax.shard_map(
        body, mesh=fine, in_specs=placed, out_specs=P(REP, None, FSDP, None), check_vma=False
    )
```

time: 84.7 us -> 80.9 us (0.955)
  local copies, waits for them, and re-layouts: 7.36 us -> 0.71 us
  Pallas kernels: 0 us -> 4.51 us
  matrix products: 1.33 us -> 0 us
    pallas_call x0 -> x2, Pallas kernels: none -> 4.51 us  [the longest x1 2.7 us: body(): pl.pallas_call(merge_kernel, out_shape=jax.ShapeDtypeStruct((N, rows, wid...]
    gather x3 -> x0, local copies, waits for them, and re-layouts: 3.58 us -> none  [the longest x1 1.38 us: body(): order = tp_order.at[f ^ swing(jnp.arange(N))].get(mode='promise_in_bounds')]
    reshape x1 -> x0, local copies, waits for them, and re-layouts: 2.06 us -> none  [body(): return wide.transpose(1, 2, 0, 3).reshape(1, *piece.shape[:2], N * width)]
    dot_general x1 -> x0, matrix products: 1.33 us -> none  [body(): jnp.dot(factor_in[0], factor_out[0], preferred_element_type=jnp.float32)]
    transpose x1 -> x0, local copies, waits for them, and re-layouts: 1.02 us -> none  [body(): return wide.transpose(1, 2, 0, 3).reshape(1, *piece.shape[:2], N * width)]
where the time goes in v3:
time: 80.9 us; the launch traced here: 80.6 us
  starting transfers between devices  33.5 us (41%)
  blocking collectives  23.3 us (29%)
  waiting for transfers between devices  18.5 us (23%)
  Pallas kernels  4.51 us (6%)
    all_to_all x1, blocking collectives, body(): lax.all_to_all(copies, ('xl', 'y'), split_axis=0, concat_axis=0, tiled=True)  23.3 us
    all_to_all x1, starting transfers between devices, body(): parts = lax.all_to_all(blocks, REP, split_axis=0, concat_axis=0, tiled=True)  17.7 us
    all_to_all x1, waiting for transfers between devices, body(): parts = lax.all_to_all(blocks, REP, split_axis=0, concat_axis=0, tiled=True)  14.2 us
    ppermute x1, starting transfers between devices, body(): piece = lax.ppermute(chosen, EVERY, pairs)  11 us
    ppermute x1, starting transfers between devices, body(): other = lax.ppermute(half, 'c', [(0, 1), (1, 0)])  4.82 us
    pallas_call x1, Pallas kernels, body(): pl.pallas_call(merge_kernel, out_shape=jax.ShapeDtypeStruct((N, rows, wid...  2.7 us
    ppermute x1, waiting for transfers between devices, body(): piece = lax.ppermute(chosen, EVERY, pairs)  2.55 us
    pallas_call x1, Pallas kernels, body(): pl.pallas_call(order_kernel, out_shape=jax.ShapeDtypeStruct((*piece.shape...  1.81 us
  transfers between devices with their start and end apart: 3, of which 3 were waited for; matrix products, arithmetic and copies ran while one was open for 0% of the time, Pallas kernels for 0%

profile of v3, /device:TPU:1, one launch (start us, length us, event | category | flops | bytes accessed | tf_op | source)
XLA Modules:
  0.0 80.6 jit_solution(310010606884609812)
XLA Ops:
  0.0 0.0 copy-start
  0.0 2.7 %merge.1 = bf16[32,48,128]{2,1,0:T(8,128)(2,1)} custom-call(s32[1]{0:T(128)} %bitcast.2.me, s32[32]{0:T(128)} %tp_order.1, bf16[1536,128]{1,0:T(8,128)(2,1)} %bitcast.9, bf16[32,1536]{1,0:T(8,128)(2,1)} %bitcast.10, bf16[32,128]{1,0:T(8,128)(2,1)} %bitcast.11), custom_call_target="tpu_custom_call" | custom-call | tf_op jit(solution)/shard_map/merge/pallas_call | solution.py:69
  2.7 17.7 %all-to-all-start = ((bf16[32,48,128]{2,1,0:T(8,128)(2,1)}), bf16[32,48,128]{2,1,0:T(8,128)(2,1)S(1)}, u32[]{:S(2)}, u32[]{:S(2)}) async-start(bf16[32,48,128]{2,1,0:T(8,128)(2,1)} %merge.1), calls=%async_computation | async-start | bytes 786432 | tf_op jit(solution)/shard_map/all_to_all | solution.py:85
  20.4 0.0 copy-done
  20.4 14.2 %all-to-all-done = bf16[32,48,128]{2,1,0:T(8,128)(2,1)S(1)} async-done(((bf16[32,48,128]{2,1,0:T(8,128)(2,1)}), bf16[32,48,128]{2,1,0:T(8,128)(2,1)S(1)}, u32[]{:S(2)}, u32[]{:S(2)}) %all-to-all-start) | async-done | bytes 393248 | tf_op jit(solution)/shard_map/all_to_all | solution.py:85
  34.6 0.6 gather_fusion
  35.1 11.0 %collective-permute-start = (bf16[4,48,128]{2,1,0:T(8,128)(2,1)S(1)}, bf16[4,48,128]{2,1,0:T(8,128)(2,1)S(1)}, u32[]{:S(2)}, u32[]{:S(2)}) collective-permute-start(bf16[4,48,128]{2,1,0:T(8,128)(2,1)S(1)} %gather_fusion), channel_id=1, source_target_pairs={{0,0},{1,513},{2,66},{3,579},{4,132},{5,645},{6,198},{7,711},{8,26... | collective-permute-start | bytes 147464 | tf_op jit(solution)/shard_map/ppermute | solution.py:88
  46.1 2.6 %collective-permute-done = bf16[4,48,128]{2,1,0:T(8,128)(2,1)S(1)} collective-permute-done((bf16[4,48,128]{2,1,0:T(8,128)(2,1)S(1)}, bf16[4,48,128]{2,1,0:T(8,128)(2,1)S(1)}, u32[]{:S(2)}, u32[]{:S(2)}) %collective-permute-start) | collective-permute-done | bytes 49184 | tf_op jit(solution)/shard_map/ppermute | solution.py:88
  48.7 0.1 broadcast_in_dim.17
  48.8 23.3 %all_to_all.10.own = bf16[16,4,48,128]{3,2,1,0:T(8,128)(2,1)S(1)} all-to-all(bf16[16,4,48,128]{3,2,1,0:T(8,128)(2,1)S(1)} %broadcast_in_dim.17), channel_id=1, replica_groups=mesh['z'=16,'xh'=2,'xl'=2,'y'=8,'c'=2] {'xl','y'}, dimensions={0} | all-to-all | bytes 1572864 | tf_op jit(solution)/shard_map/all_to_all | solution.py:90
  72.1 4.8 %collective-permute-start.1 = (bf16[16,4,48,128]{3,2,1,0:T(8,128)(2,1)S(1)}, bf16[16,4,48,128]{3,2,1,0:T(8,128)(2,1)S(1)}, u32[]{:S(2)}, u32[]{:S(2)}) collective-permute-start(bf16[16,4,48,128]{3,2,1,0:T(8,128)(2,1)S(1)} %all_to_all.10.own), channel_id=1, source_target_pairs={{0,1},{1,0},{2,3},{3,2},{4,5},{5,4},{6,7},{7,6},{8,9},{9,8},{10,11... | collective-permute-start | bytes 2359304 | tf_op jit(solution)/shard_map/ppermute | solution.py:91
  76.9 0.1 pad_add_fusion.me
  77.0 1.8 %collective-permute-done.1.other = bf16[16,4,48,128]{3,2,1,0:T(8,128)(2,1)S(1)} collective-permute-done((bf16[16,4,48,128]{3,2,1,0:T(8,128)(2,1)S(1)}, bf16[16,4,48,128]{3,2,1,0:T(8,128)(2,1)S(1)}, u32[]{:S(2)}, u32[]{:S(2)}) %collective-permute-start.1) | collective-permute-done | bytes 786464 | tf_op jit(solution)/shard_map/ppermute | solution.py:91
  78.8 1.8 %order.1 = bf16[4,48,4096]{2,1,0:T(8,128)(2,1)} custom-call(s32[2]{0:T(128)S(1)} %pad_add_fusion.me, bf16[16,4,48,128]{3,2,1,0:T(8,128)(2,1)S(1)} %all_to_all.10.own, bf16[16,4,48,128]{3,2,1,0:T(8,128)(2,1)S(1)} %collective-permute-done.1.other), custom_call_target="tpu_custom_call" | custom-call | tf_op jit(solution)/shard_map/order/pallas_call | solution.py:92
  (2 shorter events, 0.0 us)
Async XLA Ops:
  0.0 20.4 %copy-start = (s32[4]{0:T(128)S(1)}, s32[4]{0:T(128)}, u32[]{:S(2)}) copy-start(s32[4]{0:T(128)} %param.8) | copy-start | bytes 52
  2.7 31.9 %all-to-all-start = ((bf16[32,48,128]{2,1,0:T(8,128)(2,1)}), bf16[32,48,128]{2,1,0:T(8,128)(2,1)S(1)}, u32[]{:S(2)}, u32[]{:S(2)}) async-start(bf16[32,48,128]{2,1,0:T(8,128)(2,1)} %merge.1), calls=%async_computation | async-start | bytes 786432 | tf_op jit(solution)/shard_map/all_to_all | solution.py:85
  35.1 13.5 %collective-permute-start = (bf16[4,48,128]{2,1,0:T(8,128)(2,1)S(1)}, bf16[4,48,128]{2,1,0:T(8,128)(2,1)S(1)}, u32[]{:S(2)}, u32[]{:S(2)}) collective-permute-start(bf16[4,48,128]{2,1,0:T(8,128)(2,1)S(1)} %gather_fusion), channel_id=1, source_target_pairs={{0,0},{1,513},{2,66},{3,579},{4,132},{5,645},{6,198},{7,711},{8,26... | collective-permute-start | bytes 147464 | tf_op jit(solution)/shard_map/ppermute | solution.py:88
  72.1 6.7 %collective-permute-start.1 = (bf16[16,4,48,128]{3,2,1,0:T(8,128)(2,1)S(1)}, bf16[16,4,48,128]{3,2,1,0:T(8,128)(2,1)S(1)}, u32[]{:S(2)}, u32[]{:S(2)}) collective-permute-start(bf16[16,4,48,128]{3,2,1,0:T(8,128)(2,1)S(1)} %all_to_all.10.own), channel_id=1, source_target_pairs={{0,1},{1,0},{2,3},{3,2},{4,5},{5,4},{6,7},{7,6},{8,9},{9,8},{10,11... | collective-permute-start | bytes 2359304 | tf_op jit(solution)/shard_map/ppermute | solution.py:91

commit v4 on v3

--- a/solution.py
+++ b/solution.py
@@ -15,9 +15,12 @@
 LOCAL = pl.BlockSpec(memory_space=pltpu.VMEM)
 
 
+NEAR = (0, 1, 2, 3, 4, 5, 6, 7, 8, 9, 10, 12, 22, 24, 25, 26)
+CODES = (NEAR, tuple(d for d in range(N) if d not in NEAR))
+
+
 def swing(r):
-    xl, y, c = r // 16, (r // 2) % 8, r % 2
-    return (c * 8 + y) * 2 + xl
+    return CODES[r % 2][r // 2]
 
 
 def merge_kernel(me, tp_order, base, left, right, out, tp, rows_in, a, b, merged, sems, tp_sem):
@@ -54,9 +57,8 @@
     width = own.shape[-1]
     for k in range(own.shape[1]):
         for at in range(own.shape[0]):
-            code = (at % 8) * 2 + at // 8
             for side, ref in enumerate((own, other)):
-                lane = pl.multiple_of((me[side] ^ code) * width, width)
+                lane = pl.multiple_of(me[side, at] * width, width)
                 wide[k, :, pl.ds(lane, width)] = ref[at, k]
         pltpu.make_async_copy(wide.at[k], out.at[k], sems.at[k]).start()
     for k in range(own.shape[1]):
@@ -100,7 +102,7 @@
         ],
         compiler_params=pltpu.CompilerParams(vmem_limit_bytes=8 << 20),
         name="order",
-    )(jnp.stack([f ^ (c * 16), f ^ ((1 - c) * 16)]), half, other)
+    )(f ^ jnp.where(c == 0, jnp.array(CODES), jnp.array(CODES[::-1])), half, other)
     return out[None]
 
 

time: 80.9 us -> 81.4 us (level)
  starting transfers between devices: 33.5 us -> 26.2 us
  blocking collectives: 23.3 us -> 27.7 us
  waiting for transfers between devices: 18.5 us -> 21.9 us
    ppermute x1, starting transfers between devices: 11 us -> 6.52 us  [body(): piece = lax.ppermute(chosen, EVERY, pairs)]
    all_to_all x1, blocking collectives: 23.3 us -> 27.7 us  [body(): lax.all_to_all(copies, ('xl', 'y'), split_axis=0, concat_axis=0, tiled=True)]
    ppermute x1, waiting for transfers between devices: 2.55 us -> 5.61 us  [body(): piece = lax.ppermute(chosen, EVERY, pairs)]
    ppermute x1, starting transfers between devices: 4.82 us -> 2 us  [body(): other = lax.ppermute(half, 'c', [(0, 1), (1, 0)])]
where the time goes in v4:
time: 81.4 us; the launch traced here: 81.1 us
  blocking collectives  27.7 us (34%)
  starting transfers between devices  26.2 us (32%)
  waiting for transfers between devices  21.9 us (27%)
  Pallas kernels  4.5 us (6%)
    all_to_all x1, blocking collectives, body(): lax.all_to_all(copies, ('xl', 'y'), split_axis=0, concat_axis=0, tiled=True)  27.7 us
    all_to_all x1, starting transfers between devices, body(): parts = lax.all_to_all(blocks, REP, split_axis=0, concat_axis=0, tiled=True)  17.7 us
    all_to_all x1, waiting for transfers between devices, body(): parts = lax.all_to_all(blocks, REP, split_axis=0, concat_axis=0, tiled=True)  14.2 us
    ppermute x1, starting transfers between devices, body(): piece = lax.ppermute(chosen, EVERY, pairs)  6.52 us
    ppermute x1, waiting for transfers between devices, body(): piece = lax.ppermute(chosen, EVERY, pairs)  5.61 us
    pallas_call x1, Pallas kernels, body(): pl.pallas_call(merge_kernel, out_shape=jax.ShapeDtypeStruct((N, rows, wid...  2.7 us
    ppermute x1, waiting for transfers between devices, body(): other = lax.ppermute(half, 'c', [(0, 1), (1, 0)])  2.13 us
    ppermute x1, starting transfers between devices, body(): other = lax.ppermute(half, 'c', [(0, 1), (1, 0)])  2 us
  transfers between devices with their start and end apart: 3, of which 3 were waited for; matrix products, arithmetic and copies ran while one was open for 0% of the time, Pallas kernels for 0%

profile of v4, /device:TPU:1, one launch (start us, length us, event | category | flops | bytes accessed | tf_op | source)
XLA Modules:
  0.0 81.1 jit_solution(9296589230726076207)
XLA Ops:
  0.0 0.0 copy-start.2
  0.0 2.7 %merge.1 = bf16[32,48,128]{2,1,0:T(8,128)(2,1)} custom-call(s32[1]{0:T(128)} %bitcast.me, s32[32]{0:T(128)} %tp_order.1, bf16[1536,128]{1,0:T(8,128)(2,1)} %bitcast.7, bf16[32,1536]{1,0:T(8,128)(2,1)} %bitcast.8, bf16[32,128]{1,0:T(8,128)(2,1)} %bitcast.9), custom_call_target="tpu_custom_call" | custom-call | tf_op jit(solution)/shard_map/merge/pallas_call | solution.py:71
  2.7 0.0 copy-start
  2.7 0.0 copy-start.1
  2.7 17.7 %all-to-all-start = ((bf16[32,48,128]{2,1,0:T(8,128)(2,1)}), bf16[32,48,128]{2,1,0:T(8,128)(2,1)S(1)}, u32[]{:S(2)}, u32[]{:S(2)}) async-start(bf16[32,48,128]{2,1,0:T(8,128)(2,1)} %merge.1), calls=%async_computation | async-start | bytes 786432 | tf_op jit(solution)/shard_map/all_to_all | solution.py:87
  20.4 0.0 copy-done.2
  20.4 14.2 %all-to-all-done = bf16[32,48,128]{2,1,0:T(8,128)(2,1)S(1)} async-done(((bf16[32,48,128]{2,1,0:T(8,128)(2,1)}), bf16[32,48,128]{2,1,0:T(8,128)(2,1)S(1)}, u32[]{:S(2)}, u32[]{:S(2)}) %all-to-all-start) | async-done | bytes 393248 | tf_op jit(solution)/shard_map/all_to_all | solution.py:87
  34.6 0.6 gather_fusion
  35.2 6.5 %collective-permute-start = (bf16[4,48,128]{2,1,0:T(8,128)(2,1)S(1)}, bf16[4,48,128]{2,1,0:T(8,128)(2,1)S(1)}, u32[]{:S(2)}, u32[]{:S(2)}) collective-permute-start(bf16[4,48,128]{2,1,0:T(8,128)(2,1)S(1)} %gather_fusion), channel_id=1, source_target_pairs={{0,0},{1,353},{2,34},{3,419},{4,68},{5,453},{6,102},{7,487},{8,136... | collective-permute-start | bytes 147464 | tf_op jit(solution)/shard_map/ppermute | solution.py:90
  41.7 5.6 %collective-permute-done = bf16[4,48,128]{2,1,0:T(8,128)(2,1)S(1)} collective-permute-done((bf16[4,48,128]{2,1,0:T(8,128)(2,1)S(1)}, bf16[4,48,128]{2,1,0:T(8,128)(2,1)S(1)}, u32[]{:S(2)}, u32[]{:S(2)}) %collective-permute-start) | collective-permute-done | bytes 49184 | tf_op jit(solution)/shard_map/ppermute | solution.py:90
  47.3 0.1 broadcast_in_dim.17
  47.4 27.7 %all_to_all.10.own = bf16[16,4,48,128]{3,2,1,0:T(8,128)(2,1)S(1)} all-to-all(bf16[16,4,48,128]{3,2,1,0:T(8,128)(2,1)S(1)} %broadcast_in_dim.17), channel_id=1, replica_groups=mesh['z'=16,'xh'=2,'xl'=2,'y'=8,'c'=2] {'xl','y'}, dimensions={0} | all-to-all | bytes 1572864 | tf_op jit(solution)/shard_map/all_to_all | solution.py:92
  75.2 2.0 %collective-permute-start.1 = (bf16[16,4,48,128]{3,2,1,0:T(8,128)(2,1)S(1)}, bf16[16,4,48,128]{3,2,1,0:T(8,128)(2,1)S(1)}, u32[]{:S(2)}, u32[]{:S(2)}) collective-permute-start(bf16[16,4,48,128]{3,2,1,0:T(8,128)(2,1)S(1)} %all_to_all.10.own), channel_id=1, source_target_pairs={{0,1},{1,0},{2,3},{3,2},{4,5},{5,4},{6,7},{7,6},{8,9},{9,8},{10,11... | collective-permute-start | bytes 2359304 | tf_op jit(solution)/shard_map/ppermute | solution.py:93
  77.2 0.0 copy-done
  77.2 0.0 copy-done.1
  77.2 2.1 %collective-permute-done.1.other = bf16[16,4,48,128]{3,2,1,0:T(8,128)(2,1)S(1)} collective-permute-done((bf16[16,4,48,128]{3,2,1,0:T(8,128)(2,1)S(1)}, bf16[16,4,48,128]{3,2,1,0:T(8,128)(2,1)S(1)}, u32[]{:S(2)}, u32[]{:S(2)}) %collective-permute-start.1) | collective-permute-done | bytes 786464 | tf_op jit(solution)/shard_map/ppermute | solution.py:93
  79.3 1.8 %order.1 = bf16[4,48,4096]{2,1,0:T(8,128)(2,1)} custom-call(s32[2,16]{1,0:T(2,128)S(1)} %select_xor_fusion.me, bf16[16,4,48,128]{3,2,1,0:T(8,128)(2,1)S(1)} %all_to_all.10.own, bf16[16,4,48,128]{3,2,1,0:T(8,128)(2,1)S(1)} %collective-permute-done.1.other), custom_call_target="tpu_custom_call" | custom-call | tf_op jit(solution)/shard_map/order/pallas_call | solution.py:94
  (3 shorter events, 0.0 us)
Async XLA Ops:
  0.0 20.4 %copy-start.2 = (s32[4]{0:T(128)S(1)}, s32[4]{0:T(128)}, u32[]{:S(2)}) copy-start(s32[4]{0:T(128)} %param.10) | copy-start | bytes 52
  2.7 74.4 %copy-start = (s32[2,16]{1,0:T(2,128)S(1)}, s32[2,16]{1,0:T(2,128)}, u32[]{:S(2)}) copy-start(s32[2,16]{1,0:T(2,128)} %constant.26.clone) | copy-start | bytes 388
  2.7 74.4 %copy-start.1 = (s32[2,16]{1,0:T(2,128)S(1)}, s32[2,16]{1,0:T(2,128)}, u32[]{:S(2)}) copy-start(s32[2,16]{1,0:T(2,128)} %constant.25.clone) | copy-start | bytes 388
  2.7 31.9 %all-to-all-start = ((bf16[32,48,128]{2,1,0:T(8,128)(2,1)}), bf16[32,48,128]{2,1,0:T(8,128)(2,1)S(1)}, u32[]{:S(2)}, u32[]{:S(2)}) async-start(bf16[32,48,128]{2,1,0:T(8,128)(2,1)} %merge.1), calls=%async_computation | async-start | bytes 786432 | tf_op jit(solution)/shard_map/all_to_all | solution.py:87
  35.2 12.1 %collective-permute-start = (bf16[4,48,128]{2,1,0:T(8,128)(2,1)S(1)}, bf16[4,48,128]{2,1,0:T(8,128)(2,1)S(1)}, u32[]{:S(2)}, u32[]{:S(2)}) collective-permute-start(bf16[4,48,128]{2,1,0:T(8,128)(2,1)S(1)} %gather_fusion), channel_id=1, source_target_pairs={{0,0},{1,353},{2,34},{3,419},{4,68},{5,453},{6,102},{7,487},{8,136... | collective-permute-start | bytes 147464 | tf_op jit(solution)/shard_map/ppermute | solution.py:90
  75.2 4.2 %collective-permute-start.1 = (bf16[16,4,48,128]{3,2,1,0:T(8,128)(2,1)S(1)}, bf16[16,4,48,128]{3,2,1,0:T(8,128)(2,1)S(1)}, u32[]{:S(2)}, u32[]{:S(2)}) collective-permute-start(bf16[16,4,48,128]{3,2,1,0:T(8,128)(2,1)S(1)} %all_to_all.10.own), channel_id=1, source_target_pairs={{0,1},{1,0},{2,3},{3,2},{4,5},{5,4},{6,7},{7,6},{8,9},{9,8},{10,11... | collective-permute-start | bytes 2359304 | tf_op jit(solution)/shard_map/ppermute | solution.py:93

commit v5 on v3

v5 whole, which is shorter than its diff:
```python
import jax
import jax.numpy as jnp
from jax import lax
from jax.experimental import pallas as pl
from jax.experimental.pallas import tpu as pltpu
from jax.sharding import Mesh, PartitionSpec as P

ADAPTER_SCALING = 2.0
CUT = {"z": 16, "xh": 2, "xl": 2, "yh": 2, "yl": 4, "c": 2}
FSDP, REP = ("z", "xh"), ("xl", "yh", "yl", "c")
VISIT = ("yl", "yh", "xl", "c")
EVERY = FSDP + REP
N = 32
SCALAR = pl.BlockSpec(memory_space=pltpu.SMEM)
FAR = pl.BlockSpec(memory_space=pl.ANY)
LOCAL = pl.BlockSpec(memory_space=pltpu.VMEM)


def swing(r):
    xl, y, c = r // 16, (r // 2) % 8, r % 2
    return (c * 8 + y) * 2 + xl


def stop(r):
    xl, yh, yl, c = r // 16, r // 8 % 2, r // 2 % 4, r % 2
    return ((yl * 2 + yh) * 2 + xl) * 2 + c


def merge_kernel(me, tp_order, base, left, right, out, tp, slot, rows_in, a, b, merged, *sems):
    in_sems, out_sems, tp_sem = sems
    step, rows = 384, out.shape[1]
    parts = [pl.ds(at, step) for at in range(0, base.shape[0], step)]
    order = pltpu.make_async_copy(tp_order, tp, tp_sem)
    moves = [
        pltpu.make_async_copy(left, a, in_sems.at[0]),
        pltpu.make_async_copy(right, b, in_sems.at[1]),
    ] + [
        pltpu.make_async_copy(base.at[part], rows_in.at[part], in_sems.at[2 + i])
        for i, part in enumerate(parts)
    ]
    order.start()
    for move in moves:
        move.start()
    order.wait()
    for r in range(N):
        slot[tp[me[0] ^ swing(r)]] = stop(r)
    for move in moves[:2]:
        move.wait()
    sent = []
    for part, move in zip(parts, moves[2:]):
        delta = lax.dot_general(
            a[:, part], b[...], (((0,), (0,)), ((), ())), preferred_element_type=jnp.float32
        )
        move.wait()
        wide = rows_in[part, :].astype(jnp.float32) + ADAPTER_SCALING * delta
        merged[part, :] = wide.astype(jnp.bfloat16)
        for t in range(part.start // rows, (part.start + step) // rows):
            block = merged.at[pl.ds(t * rows, rows)]
            sent.append(pltpu.make_async_copy(block, out.at[slot[t]], out_sems.at[t]))
            sent[-1].start()
    for move in sent:
        move.wait()


def order_kernel(me, pieces, *refs):
    out, wide, sems = refs[-3:]
    width, half = pieces.shape[-1], wide.shape[-1]
    place = pl.ds(pl.multiple_of(me[0] // 16 * half, half), half)
    moves = []
    for k in range(pieces.shape[1]):
        for at in range(pieces.shape[0]):
            code = (at % 8) * 2 + at // 8
            lane = pl.multiple_of((me[0] % 16 ^ code) * width, width)
            wide[k, :, pl.ds(lane, width)] = pieces[at, k]
        moves.append(pltpu.make_async_copy(wide.at[k], out.at[k, :, place], sems.at[k]))
        moves[-1].start()
    for move in moves:
        move.wait()


def order(me, pieces, sofar=None):
    _, buckets, rows, width = pieces.shape
    return pl.pallas_call(
        order_kernel,
        out_shape=jax.ShapeDtypeStruct((buckets, rows, N * width), jnp.bfloat16),
        in_specs=[SCALAR, LOCAL] + [FAR] * (sofar is not None),
        out_specs=FAR,
        scratch_shapes=[
            pltpu.VMEM((buckets, rows, N // 2 * width), jnp.bfloat16),
            pltpu.SemaphoreType.DMA((buckets,)),
        ],
        input_output_aliases={} if sofar is None else {2: 0},
        compiler_params=pltpu.CompilerParams(vmem_limit_bytes=8 << 20),
        name="order",
    )(*([me[None], pieces] if sofar is None else [me[None], pieces, sofar]))


def body(base, factor_in, factor_out, source_group, tp_order):
    f, c = lax.axis_index(FSDP), lax.axis_index("c")
    rows, width = base.shape[1] // N, base.shape[2]
    blocks = pl.pallas_call(
        merge_kernel,
        out_shape=jax.ShapeDtypeStruct((N, rows, width), jnp.bfloat16),
        in_specs=[SCALAR] + [FAR] * 4,
        out_specs=FAR,
        scratch_shapes=[
            pltpu.SMEM((N,), jnp.int32),
            pltpu.SMEM((N,), jnp.int32),
            pltpu.VMEM((N * rows, width), jnp.bfloat16),
            pltpu.VMEM(factor_in.shape[:0:-1], jnp.bfloat16),
            pltpu.VMEM(factor_out.shape[1:], jnp.bfloat16),
            pltpu.VMEM((N * rows, width), jnp.bfloat16),
            pltpu.SemaphoreType.DMA((6,)),
            pltpu.SemaphoreType.DMA((N,)),
            pltpu.SemaphoreType.DMA(()),
        ],
        name="merge",
    )(f[None], tp_order, base[0], factor_in[0].T, factor_out[0])
    parts = lax.all_to_all(blocks, VISIT, split_axis=0, concat_axis=0, tiled=True)
    chosen = parts.at[stop(source_group)].get(mode="promise_in_bounds")
    pairs = [(s * N + r, (s ^ swing(r)) * N + r) for s in range(N) for r in range(N)]
    piece = lax.ppermute(chosen, EVERY, pairs)
    copies = jnp.broadcast_to(piece[None], (16, *piece.shape))
    half = lax.all_to_all(copies, ("xl", "yh", "yl"), split_axis=0, concat_axis=0, tiled=True)
    other = lax.ppermute(half, "c", [(0, 1), (1, 0)])
    out = order(f ^ (c * 16), half)
    out = order(f ^ ((1 - c) * 16), other, out)
    return out[None]


def solution(mesh):
    fine = Mesh(mesh.devices.reshape(tuple(CUT.values())), tuple(CUT))
    placed = (P(REP, None, FSDP), P(REP, None, None), P(REP, None, FSDP), P(), P())
    return jax.shard_map(
        body, mesh=fine, in_specs=placed, out_specs=P(REP, None, FSDP, None), check_vma=False
    )
```

time: 80.9 us -> 80.8 us (level)
  blocking collectives: 23.3 us -> 26 us
  waiting for transfers between devices: 18.5 us -> 16.1 us
    all_to_all x1, blocking collectives: 23.3 us -> 26 us  [body(): lax.all_to_all(copies, ('xl', 'yh', 'yl'), split_axis=0, concat_axis=0, t...]
    all_to_all x1, waiting for transfers between devices: 14.2 us -> 12.8 us  [body(): lax.all_to_all(blocks, VISIT, split_axis=0, concat_axis=0, tiled=True)]
    ppermute x1, waiting for transfers between devices: 1.8 us -> 0.92 us  [body(): other = lax.ppermute(half, 'c', [(0, 1), (1, 0)])]
    pallas_call x1 -> x2, Pallas kernels: 1.81 us -> 1.9 us  [order(): pl.pallas_call(order_kernel, out_shape=jax.ShapeDtypeStruct((buckets, row...]
  transfers between devices with their start and end apart: 3 -> 3, of which waited for: 3 -> 3; matrix products, arithmetic and copies ran while one was open for 0% -> 0% of each run, Pallas kernels for 0% -> 1%
where the time goes in v5:
time: 80.8 us; the launch traced here: 80.5 us
  starting transfers between devices  33 us (41%)
  blocking collectives  26 us (32%)
  waiting for transfers between devices  16.1 us (20%)
  Pallas kernels  4.69 us (6%)
    all_to_all x1, blocking collectives, body(): lax.all_to_all(copies, ('xl', 'yh', 'yl'), split_axis=0, concat_axis=0, t...  26 us
    all_to_all x1, starting transfers between devices, body(): lax.all_to_all(blocks, VISIT, split_axis=0, concat_axis=0, tiled=True)  17.7 us
    all_to_all x1, waiting for transfers between devices, body(): lax.all_to_all(blocks, VISIT, split_axis=0, concat_axis=0, tiled=True)  12.8 us
    ppermute x1, starting transfers between devices, body(): piece = lax.ppermute(chosen, EVERY, pairs)  11.2 us
    ppermute x1, starting transfers between devices, body(): other = lax.ppermute(half, 'c', [(0, 1), (1, 0)])  4.11 us
    pallas_call x1, Pallas kernels, body(): pl.pallas_call(merge_kernel, out_shape=jax.ShapeDtypeStruct((N, rows, wid...  2.79 us
    ppermute x1, waiting for transfers between devices, body(): piece = lax.ppermute(chosen, EVERY, pairs)  2.35 us
    pallas_call x2, Pallas kernels, order(): pl.pallas_call(order_kernel, out_shape=jax.ShapeDtypeStruct((buckets, row...  1.9 us
  transfers between devices with their start and end apart: 3, of which 3 were waited for; matrix products, arithmetic and copies ran while one was open for 0% of the time, Pallas kernels for 1%

profile of v5, /device:TPU:1, one launch (start us, length us, event | category | flops | bytes accessed | tf_op | source)
XLA Modules:
  0.0 80.5 jit_solution(17685852144908492888)
XLA Ops:
  0.0 0.0 copy-start
  0.0 2.8 %merge.1 = bf16[32,48,128]{2,1,0:T(8,128)(2,1)} custom-call(s32[1]{0:T(128)} %bitcast.1.me, s32[32]{0:T(128)} %tp_order.1, bf16[1536,128]{1,0:T(8,128)(2,1)} %bitcast.9, bf16[32,1536]{1,0:T(8,128)(2,1)} %bitcast.10, bf16[32,128]{1,0:T(8,128)(2,1)} %bitcast.11), custom_call_target="tpu_custom_call" | custom-call | tf_op jit(solution)/shard_map/merge/pallas_call | solution.py:101
  2.8 17.7 %all-to-all-start = ((bf16[32,48,128]{2,1,0:T(8,128)(2,1)}), bf16[32,48,128]{2,1,0:T(8,128)(2,1)S(1)}, u32[]{:S(2)}, u32[]{:S(2)}) async-start(bf16[32,48,128]{2,1,0:T(8,128)(2,1)} %merge.1), calls=%async_computation | async-start | bytes 786432 | tf_op jit(solution)/shard_map/all_to_all | solution.py:119
  20.5 0.0 copy-done
  20.5 12.8 %all-to-all-done = bf16[32,48,128]{2,1,0:T(8,128)(2,1)S(1)} async-done(((bf16[32,48,128]{2,1,0:T(8,128)(2,1)}), bf16[32,48,128]{2,1,0:T(8,128)(2,1)S(1)}, u32[]{:S(2)}, u32[]{:S(2)}) %all-to-all-start) | async-done | bytes 393248 | tf_op jit(solution)/shard_map/all_to_all | solution.py:119
  33.3 0.6 gather_fusion
  33.9 11.2 %collective-permute-start = (bf16[4,48,128]{2,1,0:T(8,128)(2,1)S(1)}, bf16[4,48,128]{2,1,0:T(8,128)(2,1)S(1)}, u32[]{:S(2)}, u32[]{:S(2)}) collective-permute-start(bf16[4,48,128]{2,1,0:T(8,128)(2,1)S(1)} %gather_fusion), channel_id=1, source_target_pairs={{0,0},{1,513},{2,66},{3,579},{4,132},{5,645},{6,198},{7,711},{8,26... | collective-permute-start | bytes 147464 | tf_op jit(solution)/shard_map/ppermute | solution.py:122
  45.1 2.3 %collective-permute-done = bf16[4,48,128]{2,1,0:T(8,128)(2,1)S(1)} collective-permute-done((bf16[4,48,128]{2,1,0:T(8,128)(2,1)S(1)}, bf16[4,48,128]{2,1,0:T(8,128)(2,1)S(1)}, u32[]{:S(2)}, u32[]{:S(2)}) %collective-permute-start) | collective-permute-done | bytes 49184 | tf_op jit(solution)/shard_map/ppermute | solution.py:122
  47.4 0.1 broadcast_in_dim.24
  47.6 26.0 %all_to_all.10.pieces = bf16[16,4,48,128]{3,2,1,0:T(8,128)(2,1)S(1)} all-to-all(bf16[16,4,48,128]{3,2,1,0:T(8,128)(2,1)S(1)} %broadcast_in_dim.24), channel_id=1, replica_groups=mesh['z'=16,'xh'=2,'xl'=2,'yh'=2,'yl'=4,'c'=2] {'xl','yh','yl'}, dimensions={0} | all-to-all | bytes 1572864 | tf_op jit(solution)/shard_map/all_to_all | solution.py:124
  73.5 4.1 %collective-permute-start.1 = (bf16[16,4,48,128]{3,2,1,0:T(8,128)(2,1)S(1)}, bf16[16,4,48,128]{3,2,1,0:T(8,128)(2,1)S(1)}, u32[]{:S(2)}, u32[]{:S(2)}) collective-permute-start(bf16[16,4,48,128]{3,2,1,0:T(8,128)(2,1)S(1)} %all_to_all.10.pieces), channel_id=1, source_target_pairs={{0,1},{1,0},{2,3},{3,2},{4,5},{5,4},{6,7},{7,6},{8,9},{9,8},{10,11... | collective-permute-start | bytes 2359304 | tf_op jit(solution)/shard_map/ppermute | solution.py:125
  77.7 1.0 %order.2.refs_0_ = bf16[4,48,4096]{2,1,0:T(8,128)(2,1)} custom-call(s32[1]{0:T(128)} %bitcast.6.me, bf16[16,4,48,128]{3,2,1,0:T(8,128)(2,1)S(1)} %all_to_all.10.pieces), custom_call_target="tpu_custom_call" | custom-call | tf_op jit(solution)/shard_map/order/pallas_call | solution.py:83
  78.6 0.9 %collective-permute-done.1.pieces = bf16[16,4,48,128]{3,2,1,0:T(8,128)(2,1)S(1)} collective-permute-done((bf16[16,4,48,128]{3,2,1,0:T(8,128)(2,1)S(1)}, bf16[16,4,48,128]{3,2,1,0:T(8,128)(2,1)S(1)}, u32[]{:S(2)}, u32[]{:S(2)}) %collective-permute-start.1) | collective-permute-done | bytes 786464 | tf_op jit(solution)/shard_map/ppermute | solution.py:125
  79.6 0.9 %order.3 = bf16[4,48,4096]{2,1,0:T(8,128)(2,1)} custom-call(s32[1]{0:T(128)} %bitcast.me, bf16[16,4,48,128]{3,2,1,0:T(8,128)(2,1)S(1)} %collective-permute-done.1.pieces, bf16[4,48,4096]{2,1,0:T(8,128)(2,1)} %order.2.refs_0_), custom_call_target="tpu_custom_call", output_to_operand_aliasing={{}: (2, {})} | custom-call | tf_op jit(solution)/shard_map/order/pallas_call | solution.py:83
  (2 shorter events, 0.0 us)
Async XLA Ops:
  0.0 20.5 %copy-start = (s32[4]{0:T(128)S(1)}, s32[4]{0:T(128)}, u32[]{:S(2)}) copy-start(s32[4]{0:T(128)} %param.8) | copy-start | bytes 52
  2.8 30.5 %all-to-all-start = ((bf16[32,48,128]{2,1,0:T(8,128)(2,1)}), bf16[32,48,128]{2,1,0:T(8,128)(2,1)S(1)}, u32[]{:S(2)}, u32[]{:S(2)}) async-start(bf16[32,48,128]{2,1,0:T(8,128)(2,1)} %merge.1), calls=%async_computation | async-start | bytes 786432 | tf_op jit(solution)/shard_map/all_to_all | solution.py:119
  33.9 13.5 %collective-permute-start = (bf16[4,48,128]{2,1,0:T(8,128)(2,1)S(1)}, bf16[4,48,128]{2,1,0:T(8,128)(2,1)S(1)}, u32[]{:S(2)}, u32[]{:S(2)}) collective-permute-start(bf16[4,48,128]{2,1,0:T(8,128)(2,1)S(1)} %gather_fusion), channel_id=1, source_target_pairs={{0,0},{1,513},{2,66},{3,579},{4,132},{5,645},{6,198},{7,711},{8,26... | collective-permute-start | bytes 147464 | tf_op jit(solution)/shard_map/ppermute | solution.py:122
  73.5 6.0 %collective-permute-start.1 = (bf16[16,4,48,128]{3,2,1,0:T(8,128)(2,1)S(1)}, bf16[16,4,48,128]{3,2,1,0:T(8,128)(2,1)S(1)}, u32[]{:S(2)}, u32[]{:S(2)}) collective-permute-start(bf16[16,4,48,128]{3,2,1,0:T(8,128)(2,1)S(1)} %all_to_all.10.pieces), channel_id=1, source_target_pairs={{0,1},{1,0},{2,3},{3,2},{4,5},{5,4},{6,7},{7,6},{8,9},{9,8},{10,11... | collective-permute-start | bytes 2359304 | tf_op jit(solution)/shard_map/ppermute | solution.py:125

commit v6 on v5

--- a/solution.py
+++ b/solution.py
@@ -16,9 +16,14 @@
 LOCAL = pl.BlockSpec(memory_space=pltpu.VMEM)
 
 
+SWING = (
+    (8, 31, 2, 26, 1, 27, 9, 29, 28, 19, 11, 23, 3, 13, 0, 16)
+    + (4, 24, 6, 25, 10, 18, 5, 22, 30, 15, 7, 21, 14, 20, 12, 17)
+)
+
+
 def swing(r):
-    xl, y, c = r // 16, (r // 2) % 8, r % 2
-    return (c * 8 + y) * 2 + xl
+    return SWING[r]
 
 
 def stop(r):
@@ -62,37 +67,30 @@
         move.wait()
 
 
-def order_kernel(me, pieces, *refs):
-    out, wide, sems = refs[-3:]
-    width, half = pieces.shape[-1], wide.shape[-1]
-    place = pl.ds(pl.multiple_of(me[0] // 16 * half, half), half)
+def order_kernel(places, pieces, *refs):
+    out, sems = refs[-2:]
+    width = pieces.shape[-1]
     moves = []
-    for k in range(pieces.shape[1]):
-        for at in range(pieces.shape[0]):
-            code = (at % 8) * 2 + at // 8
-            lane = pl.multiple_of((me[0] % 16 ^ code) * width, width)
-            wide[k, :, pl.ds(lane, width)] = pieces[at, k]
-        moves.append(pltpu.make_async_copy(wide.at[k], out.at[k, :, place], sems.at[k]))
+    for at in range(pieces.shape[0]):
+        lanes = pl.ds(pl.multiple_of(places[at] * width, width), width)
+        moves.append(pltpu.make_async_copy(pieces.at[at], out.at[:, :, lanes], sems.at[at]))
         moves[-1].start()
     for move in moves:
         move.wait()
 
 
-def order(me, pieces, sofar=None):
-    _, buckets, rows, width = pieces.shape
+def order(places, pieces, sofar=None):
+    many, buckets, rows, width = pieces.shape
     return pl.pallas_call(
         order_kernel,
         out_shape=jax.ShapeDtypeStruct((buckets, rows, N * width), jnp.bfloat16),
         in_specs=[SCALAR, LOCAL] + [FAR] * (sofar is not None),
         out_specs=FAR,
-        scratch_shapes=[
-            pltpu.VMEM((buckets, rows, N // 2 * width), jnp.bfloat16),
-            pltpu.SemaphoreType.DMA((buckets,)),
-        ],
+        scratch_shapes=[pltpu.SemaphoreType.DMA((many,))],
         input_output_aliases={} if sofar is None else {2: 0},
         compiler_params=pltpu.CompilerParams(vmem_limit_bytes=8 << 20),
         name="order",
-    )(*([me[None], pieces] if sofar is None else [me[None], pieces, sofar]))
+    )(*([places, pieces] if sofar is None else [places, pieces, sofar]))
 
 
 def body(base, factor_in, factor_out, source_group, tp_order):
@@ -123,8 +121,9 @@
     copies = jnp.broadcast_to(piece[None], (16, *piece.shape))
     half = lax.all_to_all(copies, ("xl", "yh", "yl"), split_axis=0, concat_axis=0, tiled=True)
     other = lax.ppermute(half, "c", [(0, 1), (1, 0)])
-    out = order(f ^ (c * 16), half)
-    out = order(f ^ ((1 - c) * 16), other, out)
+    codes = jnp.array((SWING[::2], SWING[1::2]))
+    out = order(f ^ jnp.where(c == 0, codes[0], codes[1]), half)
+    out = order(f ^ jnp.where(c == 0, codes[1], codes[0]), other, out)
     return out[None]
 
 

time: 80.8 us -> 81.1 us (level)
  Pallas kernels: 4.69 us -> 5.88 us
    ppermute x1, starting transfers between devices: 4.11 us -> 2.29 us  [body(): other = lax.ppermute(half, 'c', [(0, 1), (1, 0)])]
    pallas_call x2, Pallas kernels: 1.9 us -> 3.09 us  [order(): pl.pallas_call(order_kernel, out_shape=jax.ShapeDtypeStruct((buckets, row...]
    ppermute x1, starting transfers between devices: 11.2 us -> 12.2 us  [body(): piece = lax.ppermute(chosen, EVERY, pairs)]
  transfers between devices with their start and end apart: 3 -> 3, of which waited for: 3 -> 3; matrix products, arithmetic and copies ran while one was open for 0% -> 0% of each run, Pallas kernels for 1% -> 2%
where the time goes in v6:
time: 81.1 us; the launch traced here: 80.8 us
  starting transfers between devices  32.2 us (40%)
  blocking collectives  25.7 us (32%)
  waiting for transfers between devices  16.1 us (20%)
  Pallas kernels  5.88 us (7%)
    all_to_all x1, blocking collectives, body(): lax.all_to_all(copies, ('xl', 'yh', 'yl'), split_axis=0, concat_axis=0, t...  25.7 us
    all_to_all x1, starting transfers between devices, body(): lax.all_to_all(blocks, VISIT, split_axis=0, concat_axis=0, tiled=True)  17.7 us
    all_to_all x1, waiting for transfers between devices, body(): lax.all_to_all(blocks, VISIT, split_axis=0, concat_axis=0, tiled=True)  12.8 us
    ppermute x1, starting transfers between devices, body(): piece = lax.ppermute(chosen, EVERY, pairs)  12.2 us
    pallas_call x2, Pallas kernels, order(): pl.pallas_call(order_kernel, out_shape=jax.ShapeDtypeStruct((buckets, row...  3.09 us
    ppermute x1, waiting for transfers between devices, body(): piece = lax.ppermute(chosen, EVERY, pairs)  3.01 us
    pallas_call x1, Pallas kernels, body(): pl.pallas_call(merge_kernel, out_shape=jax.ShapeDtypeStruct((N, rows, wid...  2.79 us
    ppermute x1, starting transfers between devices, body(): other = lax.ppermute(half, 'c', [(0, 1), (1, 0)])  2.29 us
  transfers between devices with their start and end apart: 3, of which 3 were waited for; matrix products, arithmetic and copies ran while one was open for 0% of the time, Pallas kernels for 2%

profile of v6, /device:TPU:1, one launch (start us, length us, event | category | flops | bytes accessed | tf_op | source)
XLA Modules:
  0.0 80.8 jit_solution(2814569531010085967)
XLA Ops:
  0.0 0.0 copy-start.2
  0.0 2.8 %merge.1 = bf16[32,48,128]{2,1,0:T(8,128)(2,1)} custom-call(s32[1]{0:T(128)} %bitcast.1.me, s32[32]{0:T(128)} %tp_order.1, bf16[1536,128]{1,0:T(8,128)(2,1)} %bitcast.11, bf16[32,1536]{1,0:T(8,128)(2,1)} %bitcast.12, bf16[32,128]{1,0:T(8,128)(2,1)} %bitcast.13), custom_call_target="tpu_custom_call" | custom-call | tf_op jit(solution)/shard_map/merge/pallas_call | solution.py:99
  2.8 0.0 copy-start
  2.8 0.0 copy-start.1
  2.8 17.7 %all-to-all-start = ((bf16[32,48,128]{2,1,0:T(8,128)(2,1)}), bf16[32,48,128]{2,1,0:T(8,128)(2,1)S(1)}, u32[]{:S(2)}, u32[]{:S(2)}) async-start(bf16[32,48,128]{2,1,0:T(8,128)(2,1)} %merge.1), calls=%async_computation | async-start | bytes 786432 | tf_op jit(solution)/shard_map/all_to_all | solution.py:117
  20.5 0.0 copy-done.2
  20.5 12.8 %all-to-all-done = bf16[32,48,128]{2,1,0:T(8,128)(2,1)S(1)} async-done(((bf16[32,48,128]{2,1,0:T(8,128)(2,1)}), bf16[32,48,128]{2,1,0:T(8,128)(2,1)S(1)}, u32[]{:S(2)}, u32[]{:S(2)}) %all-to-all-start) | async-done | bytes 393248 | tf_op jit(solution)/shard_map/all_to_all | solution.py:117
  33.3 0.6 gather_fusion
  33.9 12.2 %collective-permute-start = (bf16[4,48,128]{2,1,0:T(8,128)(2,1)S(1)}, bf16[4,48,128]{2,1,0:T(8,128)(2,1)S(1)}, u32[]{:S(2)}, u32[]{:S(2)}) collective-permute-start(bf16[4,48,128]{2,1,0:T(8,128)(2,1)S(1)} %gather_fusion), channel_id=1, source_target_pairs={{0,256},{1,993},{2,66},{3,835},{4,36},{5,869},{6,294},{7,935},{8,9... | collective-permute-start | bytes 147464 | tf_op jit(solution)/shard_map/ppermute | solution.py:120
  46.1 3.0 %collective-permute-done = bf16[4,48,128]{2,1,0:T(8,128)(2,1)S(1)} collective-permute-done((bf16[4,48,128]{2,1,0:T(8,128)(2,1)S(1)}, bf16[4,48,128]{2,1,0:T(8,128)(2,1)S(1)}, u32[]{:S(2)}, u32[]{:S(2)}) %collective-permute-start) | collective-permute-done | bytes 49184 | tf_op jit(solution)/shard_map/ppermute | solution.py:120
  49.1 0.1 broadcast_in_dim.17
  49.3 25.7 %all_to_all.10.pieces = bf16[16,4,48,128]{3,2,1,0:T(8,128)(2,1)S(1)} all-to-all(bf16[16,4,48,128]{3,2,1,0:T(8,128)(2,1)S(1)} %broadcast_in_dim.17), channel_id=1, replica_groups=mesh['z'=16,'xh'=2,'xl'=2,'yh'=2,'yl'=4,'c'=2] {'xl','yh','yl'}, dimensions={0} | all-to-all | bytes 1572864 | tf_op jit(solution)/shard_map/all_to_all | solution.py:122
  75.0 2.3 %collective-permute-start.1 = (bf16[16,4,48,128]{3,2,1,0:T(8,128)(2,1)S(1)}, bf16[16,4,48,128]{3,2,1,0:T(8,128)(2,1)S(1)}, u32[]{:S(2)}, u32[]{:S(2)}) collective-permute-start(bf16[16,4,48,128]{3,2,1,0:T(8,128)(2,1)S(1)} %all_to_all.10.pieces), channel_id=1, source_target_pairs={{0,1},{1,0},{2,3},{3,2},{4,5},{5,4},{6,7},{7,6},{8,9},{9,8},{10,11... | collective-permute-start | bytes 2359304 | tf_op jit(solution)/shard_map/ppermute | solution.py:123
  77.3 0.0 copy-done
  77.4 0.0 copy-done.1
  77.4 1.5 %order.2.refs_0_ = bf16[4,48,4096]{2,1,0:T(8,128)(2,1)} custom-call(s32[16]{0:T(128)S(1)} %get-tuple-element.5.places, bf16[16,4,48,128]{3,2,1,0:T(8,128)(2,1)S(1)} %all_to_all.10.pieces), custom_call_target="tpu_custom_call" | custom-call | tf_op jit(solution)/shard_map/order/pallas_call | solution.py:84
  78.9 0.3 collective-permute-done.1.pieces
  79.2 1.5 %order.3 = bf16[4,48,4096]{2,1,0:T(8,128)(2,1)} custom-call(s32[16]{0:T(128)S(1)} %get-tuple-element.6.places, bf16[16,4,48,128]{3,2,1,0:T(8,128)(2,1)S(1)} %collective-permute-done.1.pieces, bf16[4,48,4096]{2,1,0:T(8,128)(2,1)} %order.2.refs_0_), custom_call_target="tpu_custom_call", output_to_operand_aliasing={{}: (2, {})} | custom-call | tf_op jit(solution)/shard_map/order/pallas_call | solution.py:84
  (3 shorter events, 0.0 us)
Async XLA Ops:
  0.0 20.5 %copy-start.2 = (s32[4]{0:T(128)S(1)}, s32[4]{0:T(128)}, u32[]{:S(2)}) copy-start(s32[4]{0:T(128)} %param.9) | copy-start | bytes 52
  2.8 74.5 %copy-start = (s32[1,16]{1,0:T(1,128)S(1)}, s32[1,16]{1,0:T(1,128)}, u32[]{:S(2)}) copy-start(s32[1,16]{1,0:T(1,128)} %constant.88) | copy-start | bytes 196
  2.8 74.5 %copy-start.1 = (s32[1,16]{1,0:T(1,128)S(1)}, s32[1,16]{1,0:T(1,128)}, u32[]{:S(2)}) copy-start(s32[1,16]{1,0:T(1,128)} %constant.87) | copy-start | bytes 196
  2.8 30.5 %all-to-all-start = ((bf16[32,48,128]{2,1,0:T(8,128)(2,1)}), bf16[32,48,128]{2,1,0:T(8,128)(2,1)S(1)}, u32[]{:S(2)}, u32[]{:S(2)}) async-start(bf16[32,48,128]{2,1,0:T(8,128)(2,1)} %merge.1), calls=%async_computation | async-start | bytes 786432 | tf_op jit(solution)/shard_map/all_to_all | solution.py:117
  33.9 15.2 %collective-permute-start = (bf16[4,48,128]{2,1,0:T(8,128)(2,1)S(1)}, bf16[4,48,128]{2,1,0:T(8,128)(2,1)S(1)}, u32[]{:S(2)}, u32[]{:S(2)}) collective-permute-start(bf16[4,48,128]{2,1,0:T(8,128)(2,1)S(1)} %gather_fusion), channel_id=1, source_target_pairs={{0,256},{1,993},{2,66},{3,835},{4,36},{5,869},{6,294},{7,935},{8,9... | collective-permute-start | bytes 147464 | tf_op jit(solution)/shard_map/ppermute | solution.py:120
  75.0 4.2 %collective-permute-start.1 = (bf16[16,4,48,128]{3,2,1,0:T(8,128)(2,1)S(1)}, bf16[16,4,48,128]{3,2,1,0:T(8,128)(2,1)S(1)}, u32[]{:S(2)}, u32[]{:S(2)}) collective-permute-start(bf16[16,4,48,128]{3,2,1,0:T(8,128)(2,1)S(1)} %all_to_all.10.pieces), channel_id=1, source_target_pairs={{0,1},{1,0},{2,3},{3,2},{4,5},{5,4},{6,7},{7,6},{8,9},{9,8},{10,11... | collective-permute-start | bytes 2359304 | tf_op jit(solution)/shard_map/ppermute | solution.py:123

commit v7 on v5

--- a/solution.py
+++ b/solution.py
@@ -16,9 +16,12 @@
 LOCAL = pl.BlockSpec(memory_space=pltpu.VMEM)
 
 
+LOW = (2, 4, 3, 5, 7, 1, 6, 0)
+
+
 def swing(r):
     xl, y, c = r // 16, (r // 2) % 8, r % 2
-    return (c * 8 + y) * 2 + xl
+    return (c * 8 + LOW[y]) * 2 + xl
 
 
 def stop(r):
@@ -69,7 +72,7 @@
     moves = []
     for k in range(pieces.shape[1]):
         for at in range(pieces.shape[0]):
-            code = (at % 8) * 2 + at // 8
+            code = LOW[at % 8] * 2 + at // 8
             lane = pl.multiple_of((me[0] % 16 ^ code) * width, width)
             wide[k, :, pl.ds(lane, width)] = pieces[at, k]
         moves.append(pltpu.make_async_copy(wide.at[k], out.at[k, :, place], sems.at[k]))

time: 80.8 us -> 81 us (level)
  waiting for transfers between devices: 16.1 us -> 15.2 us
    ppermute x1, waiting for transfers between devices: 2.35 us -> 1.52 us  [body(): piece = lax.ppermute(chosen, EVERY, pairs)]
where the time goes in v7:
time: 81 us; the launch traced here: 80.6 us
  starting transfers between devices  33.6 us (41%)
  blocking collectives  26.3 us (32%)
  waiting for transfers between devices  15.2 us (19%)
  Pallas kernels  4.7 us (6%)
    all_to_all x1, blocking collectives, body(): lax.all_to_all(copies, ('xl', 'yh', 'yl'), split_axis=0, concat_axis=0, t...  26.3 us
    all_to_all x1, starting transfers between devices, body(): lax.all_to_all(blocks, VISIT, split_axis=0, concat_axis=0, tiled=True)  17.7 us
    all_to_all x1, waiting for transfers between devices, body(): lax.all_to_all(blocks, VISIT, split_axis=0, concat_axis=0, tiled=True)  12.8 us
    ppermute x1, starting transfers between devices, body(): piece = lax.ppermute(chosen, EVERY, pairs)  11.2 us
    ppermute x1, starting transfers between devices, body(): other = lax.ppermute(half, 'c', [(0, 1), (1, 0)])  4.77 us
    pallas_call x1, Pallas kernels, body(): pl.pallas_call(merge_kernel, out_shape=jax.ShapeDtypeStruct((N, rows, wid...  2.79 us
    pallas_call x2, Pallas kernels, order(): pl.pallas_call(order_kernel, out_shape=jax.ShapeDtypeStruct((buckets, row...  1.91 us
  transfers between devices with their start and end apart: 3, of which 3 were waited for; matrix products, arithmetic and copies ran while one was open for 0% of the time, Pallas kernels for 1%

profile of v7, /device:TPU:1, one launch (start us, length us, event | category | flops | bytes accessed | tf_op | source)
XLA Modules:
  0.0 80.6 jit_solution(3789431738546451477)
XLA Ops:
  0.0 0.0 copy-start
  0.0 2.8 %merge.1 = bf16[32,48,128]{2,1,0:T(8,128)(2,1)} custom-call(s32[1]{0:T(128)} %bitcast.1.me, s32[32]{0:T(128)} %tp_order.1, bf16[1536,128]{1,0:T(8,128)(2,1)} %bitcast.9, bf16[32,1536]{1,0:T(8,128)(2,1)} %bitcast.10, bf16[32,128]{1,0:T(8,128)(2,1)} %bitcast.11), custom_call_target="tpu_custom_call" | custom-call | tf_op jit(solution)/shard_map/merge/pallas_call | solution.py:104
  2.8 17.7 %all-to-all-start = ((bf16[32,48,128]{2,1,0:T(8,128)(2,1)}), bf16[32,48,128]{2,1,0:T(8,128)(2,1)S(1)}, u32[]{:S(2)}, u32[]{:S(2)}) async-start(bf16[32,48,128]{2,1,0:T(8,128)(2,1)} %merge.1), calls=%async_computation | async-start | bytes 786432 | tf_op jit(solution)/shard_map/all_to_all | solution.py:122
  20.5 0.0 copy-done
  20.5 12.8 %all-to-all-done = bf16[32,48,128]{2,1,0:T(8,128)(2,1)S(1)} async-done(((bf16[32,48,128]{2,1,0:T(8,128)(2,1)}), bf16[32,48,128]{2,1,0:T(8,128)(2,1)S(1)}, u32[]{:S(2)}, u32[]{:S(2)}) %all-to-all-start) | async-done | bytes 393248 | tf_op jit(solution)/shard_map/all_to_all | solution.py:122
  33.3 0.6 gather_fusion
  33.9 11.2 %collective-permute-start = (bf16[4,48,128]{2,1,0:T(8,128)(2,1)S(1)}, bf16[4,48,128]{2,1,0:T(8,128)(2,1)S(1)}, u32[]{:S(2)}, u32[]{:S(2)}) collective-permute-start(bf16[4,48,128]{2,1,0:T(8,128)(2,1)S(1)} %gather_fusion), channel_id=1, source_target_pairs={{0,128},{1,641},{2,258},{3,771},{4,196},{5,709},{6,326},{7,839},{8... | collective-permute-start | bytes 147464 | tf_op jit(solution)/shard_map/ppermute | solution.py:125
  45.1 1.5 %collective-permute-done = bf16[4,48,128]{2,1,0:T(8,128)(2,1)S(1)} collective-permute-done((bf16[4,48,128]{2,1,0:T(8,128)(2,1)S(1)}, bf16[4,48,128]{2,1,0:T(8,128)(2,1)S(1)}, u32[]{:S(2)}, u32[]{:S(2)}) %collective-permute-start) | collective-permute-done | bytes 49184 | tf_op jit(solution)/shard_map/ppermute | solution.py:125
  46.6 0.1 broadcast_in_dim.24
  46.8 26.3 %all_to_all.10.pieces = bf16[16,4,48,128]{3,2,1,0:T(8,128)(2,1)S(1)} all-to-all(bf16[16,4,48,128]{3,2,1,0:T(8,128)(2,1)S(1)} %broadcast_in_dim.24), channel_id=1, replica_groups=mesh['z'=16,'xh'=2,'xl'=2,'yh'=2,'yl'=4,'c'=2] {'xl','yh','yl'}, dimensions={0} | all-to-all | bytes 1572864 | tf_op jit(solution)/shard_map/all_to_all | solution.py:127
  73.0 4.8 %collective-permute-start.1 = (bf16[16,4,48,128]{3,2,1,0:T(8,128)(2,1)S(1)}, bf16[16,4,48,128]{3,2,1,0:T(8,128)(2,1)S(1)}, u32[]{:S(2)}, u32[]{:S(2)}) collective-permute-start(bf16[16,4,48,128]{3,2,1,0:T(8,128)(2,1)S(1)} %all_to_all.10.pieces), channel_id=1, source_target_pairs={{0,1},{1,0},{2,3},{3,2},{4,5},{5,4},{6,7},{7,6},{8,9},{9,8},{10,11... | collective-permute-start | bytes 2359304 | tf_op jit(solution)/shard_map/ppermute | solution.py:128
  77.8 1.0 %order.2.refs_0_ = bf16[4,48,4096]{2,1,0:T(8,128)(2,1)} custom-call(s32[1]{0:T(128)} %bitcast.6.me, bf16[16,4,48,128]{3,2,1,0:T(8,128)(2,1)S(1)} %all_to_all.10.pieces), custom_call_target="tpu_custom_call" | custom-call | tf_op jit(solution)/shard_map/order/pallas_call | solution.py:86
  78.8 0.9 %collective-permute-done.1.pieces = bf16[16,4,48,128]{3,2,1,0:T(8,128)(2,1)S(1)} collective-permute-done((bf16[16,4,48,128]{3,2,1,0:T(8,128)(2,1)S(1)}, bf16[16,4,48,128]{3,2,1,0:T(8,128)(2,1)S(1)}, u32[]{:S(2)}, u32[]{:S(2)}) %collective-permute-start.1) | collective-permute-done | bytes 786464 | tf_op jit(solution)/shard_map/ppermute | solution.py:128
  79.7 1.0 %order.3 = bf16[4,48,4096]{2,1,0:T(8,128)(2,1)} custom-call(s32[1]{0:T(128)} %bitcast.me, bf16[16,4,48,128]{3,2,1,0:T(8,128)(2,1)S(1)} %collective-permute-done.1.pieces, bf16[4,48,4096]{2,1,0:T(8,128)(2,1)} %order.2.refs_0_), custom_call_target="tpu_custom_call", output_to_operand_aliasing={{}: (2, {})} | custom-call | tf_op jit(solution)/shard_map/order/pallas_call | solution.py:86
  (2 shorter events, 0.0 us)
Async XLA Ops:
  0.0 20.5 %copy-start = (s32[4]{0:T(128)S(1)}, s32[4]{0:T(128)}, u32[]{:S(2)}) copy-start(s32[4]{0:T(128)} %param.8) | copy-start | bytes 52
  2.8 30.5 %all-to-all-start = ((bf16[32,48,128]{2,1,0:T(8,128)(2,1)}), bf16[32,48,128]{2,1,0:T(8,128)(2,1)S(1)}, u32[]{:S(2)}, u32[]{:S(2)}) async-start(bf16[32,48,128]{2,1,0:T(8,128)(2,1)} %merge.1), calls=%async_computation | async-start | bytes 786432 | tf_op jit(solution)/shard_map/all_to_all | solution.py:122
  33.9 12.7 %collective-permute-start = (bf16[4,48,128]{2,1,0:T(8,128)(2,1)S(1)}, bf16[4,48,128]{2,1,0:T(8,128)(2,1)S(1)}, u32[]{:S(2)}, u32[]{:S(2)}) collective-permute-start(bf16[4,48,128]{2,1,0:T(8,128)(2,1)S(1)} %gather_fusion), channel_id=1, source_target_pairs={{0,128},{1,641},{2,258},{3,771},{4,196},{5,709},{6,326},{7,839},{8... | collective-permute-start | bytes 147464 | tf_op jit(solution)/shard_map/ppermute | solution.py:125
  73.0 6.7 %collective-permute-start.1 = (bf16[16,4,48,128]{3,2,1,0:T(8,128)(2,1)S(1)}, bf16[16,4,48,128]{3,2,1,0:T(8,128)(2,1)S(1)}, u32[]{:S(2)}, u32[]{:S(2)}) collective-permute-start(bf16[16,4,48,128]{3,2,1,0:T(8,128)(2,1)S(1)} %all_to_all.10.pieces), channel_id=1, source_target_pairs={{0,1},{1,0},{2,3},{3,2},{4,5},{5,4},{6,7},{7,6},{8,9},{9,8},{10,11... | collective-permute-start | bytes 2359304 | tf_op jit(solution)/shard_map/ppermute | solution.py:128
